TPU v7x, 32 devices: a whole 2x2x4 slice. The times are simulated.
32 devices in a mesh: seq: 2 (over y), fsdp: 16 (over z, x, core).
Axes of the slice: x: 2, y: 2, z: 4, core: 2. Of those that a mesh axis runs over, the one named last changes fastest.
Arguments:
- tokens: bfloat16 [16, 1024, 1024], P('fsdp', 'seq'), may hold values from -6 to 6
- grad_out: bfloat16 [16, 1024, 1024], P('fsdp', 'seq'), may hold values from -6 to 6
- segments: int32 [16, 1024], P('fsdp'), may hold values from 0 to 1, as said below
- padding: int32 [16, 1024], P('fsdp'), may hold values from 0 to 1, as said below
- adapter_ids: int32 [16, 1], P('fsdp'), may hold values from 0 to 7
- norm1_gain: bfloat16 [1024], P('fsdp'), may hold values from 0.5 to 1.5
- norm1_bias: bfloat16 [1024], P('fsdp'), may hold values from -1.1953125 to 1.1953125
- w_qkv: bfloat16 [1024, 3072], P('fsdp'), may hold values from -0.1875 to 0.1875
- w_proj: bfloat16 [1024, 1024], P('fsdp'), may hold values from -3 to 3
- proj_bias: bfloat16 [1024], P('fsdp'), may hold values from -1.796875 to 1.796875
- norm2_gain: bfloat16 [1024], P('fsdp'), may hold values from 0.5 to 1.5
- norm2_bias: bfloat16 [1024], P('fsdp'), may hold values from -1.1953125 to 1.1953125
- w_fc1: bfloat16 [1024, 4096], P('fsdp'), may hold values from -0.1875 to 0.1875
- fc1_bias: bfloat16 [4096], P('fsdp'), may hold values from -3 to 3
- w_fc2: bfloat16 [4096, 1024], P('fsdp'), may hold values from -0.09375 to 0.09375
- fc2_bias: bfloat16 [1024], P('fsdp'), may hold values from -1.796875 to 1.796875
- qkv_down: bfloat16 [1024, 128], replicated, may hold values from -0.1875 to 0.1875
- qkv_up: bfloat16 [128, 3072], replicated, may hold values from -1.5 to 1.5
- proj_down: bfloat16 [1024, 128], replicated, may hold values from -3 to 3
- proj_up: bfloat16 [128, 1024], replicated, may hold values from -1.5 to 1.5
- fc1_down: bfloat16 [1024, 128], replicated, may hold values from -0.1875 to 0.1875
- fc1_up: bfloat16 [128, 4096], replicated, may hold values from -1.5 to 1.5
- fc2_down: bfloat16 [4096, 128], replicated, may hold values from -0.09375 to 0.09375
- fc2_up: bfloat16 [128, 1024], replicated, may hold values from -1.5 to 1.5
Outputs:
- output: bfloat16 [16, 1024, 1024], P('fsdp', 'seq')
- grad_tokens: float32 [16, 1024, 1024], P('fsdp', 'seq')
- grad_qkv_down: float32 [1024, 128], replicated
- grad_qkv_up: float32 [128, 3072], replicated
- grad_proj_down: float32 [1024, 128], replicated
- grad_proj_up: float32 [128, 1024], replicated
- grad_fc1_down: float32 [1024, 128], replicated
- grad_fc1_up: float32 [128, 4096], replicated
- grad_fc2_down: float32 [4096, 128], replicated
- grad_fc2_up: float32 [128, 1024], replicated
Inputs may be any that keep to these rules, and one draw needn't show every extreme that they name: `segments`: in each pack the tokens with padding 1 form 1 runs of exactly 577 tokens, in order; a token's segment number is the count of runs that begin at or before it, so run s has number s and padding takes the number of the run before it, or 0. `padding`: 1 exactly on the tokens of the runs. `adapter_ids`: entry s - 1 is the adapter of run s of the pack.
All inputs are finite; a program needn't handle non-finite values.
Results may differ from a plain program's by a relative error of at most 0.014.
The roundings to bfloat16 on the way count: a program that leaves them out, or rounds other values in their place, can miss the bound.
Values may be sent and summed in bfloat16 or wider, within the bound.
A program may use at most 192 MiB of HBM per device.

v0:
```python
from functools import partial

import jax
import jax.numpy as jnp
from jax import lax
from jax.experimental import pallas as pl
from jax.experimental.pallas import tpu as pltpu
from jax.sharding import PartitionSpec as P

HEAD_DIM = 64
IMG = 577
RANK = 16
QBLOCK = 512


norm_eps = 1e-06
masked_score = -1e30


def matmul(left_side, right_side):
    return jnp.dot(left_side, right_side, preferred_element_type=jnp.float32)


def matmul_nt(left_side, right_side):
    return jnp.einsum("tk,jk->tj", left_side, right_side, preferred_element_type=jnp.float32)


def matmul_tn(left_side, right_side):
    return jnp.einsum("ti,to->io", left_side, right_side, preferred_element_type=jnp.float32)


def layer_norm(values, norm_gain, norm_shift):
    centre = jnp.mean(values, axis=-1, keepdims=True)
    centred = values - centre
    spread = jnp.mean(centred * centred, axis=-1, keepdims=True)
    return centred * lax.rsqrt(spread + norm_eps) * norm_gain + norm_shift


def norm_backward(values, norm_gain, norm_shift, grad_in):

    def apply_norm(inputs):
        return layer_norm(inputs, norm_gain, norm_shift)

    unused, pullback = jax.vjp(apply_norm, values)
    return pullback(grad_in)[0]


def selection(seg_own, image_adapters, columns):
    images = jnp.arange(image_adapters.shape[0], dtype=jnp.int32)
    image_match = seg_own[:, None] - 1 == images[None, :]
    token_adapter = jnp.sum(jnp.where(image_match, image_adapters[None, :], 0), axis=1)
    present = jnp.any(image_match, axis=1)
    column = jnp.arange(columns, dtype=jnp.int32) // RANK
    chosen = (token_adapter[:, None] == column[None, :]) & present[:, None]
    return chosen.astype(jnp.float32)


def adapter_forward(inputs_b, weight, down_map, up_map, select):
    inner_term = (matmul(inputs_b, down_map) * select).astype(jnp.bfloat16)
    return (matmul(inputs_b, weight) + matmul(inner_term, up_map), inner_term)


def adapter_backward(inputs_b, inner_term, grad_in, weight, down_map, up_map, select):
    grad_up = matmul_tn(inner_term, grad_in)
    grad_inner = (matmul_nt(grad_in, up_map) * select).astype(jnp.bfloat16)
    grad_down = matmul_tn(inputs_b, grad_inner)
    grad_inputs = matmul_nt(grad_in, weight) + matmul_nt(grad_inner, down_map)
    return (grad_inputs, grad_down, grad_up)


def block_scores(query_block, key_heads, seg_block, seg_keys, keep_keys):
    score_scale = HEAD_DIM ** (-0.5)
    scores = (
        jnp.einsum("qhd,khd->hqk", query_block, key_heads, preferred_element_type=jnp.float32)
        * score_scale
    )
    allowed = (seg_block[:, None] == seg_keys[None, :]) & (keep_keys[None, :] == 1)
    return jnp.where(allowed[None, :, :], scores, masked_score)


def split_heads(head_rows):
    all_rows = head_rows.shape[0]
    local_heads = head_rows.shape[2] // HEAD_DIM
    query_heads = head_rows[:, 0].reshape(all_rows, local_heads, HEAD_DIM)
    key_heads = head_rows[:, 1].reshape(all_rows, local_heads, HEAD_DIM)
    value_heads = head_rows[:, 2].reshape(all_rows, local_heads, HEAD_DIM)
    return (query_heads, key_heads, value_heads)


def key_window(all_rows):
    return min(all_rows, (QBLOCK + 2 * IMG - 2 + 127) // 128 * 128)


def window_start(block_index, all_rows, window):
    first = block_index * QBLOCK - (IMG - 1)
    return jnp.clip(first, 0, all_rows - window)


def attention_forward(head_rows, seg_all, keep_all):
    all_rows = head_rows.shape[0]
    block_count = all_rows // QBLOCK
    window = key_window(all_rows)
    query_heads, key_heads, value_heads = split_heads(head_rows)
    local_heads = query_heads.shape[1]

    def one_block(block_parts):
        query_block, seg_block, keep_block, block_index = block_parts
        start = window_start(block_index, all_rows, window)
        keys_near = lax.dynamic_slice_in_dim(key_heads, start, window, 0)
        values_near = lax.dynamic_slice_in_dim(value_heads, start, window, 0)
        seg_near = lax.dynamic_slice_in_dim(seg_all, start, window, 0)
        keep_near = lax.dynamic_slice_in_dim(keep_all, start, window, 0)
        scores = block_scores(query_block, keys_near, seg_block, seg_near, keep_near)
        row_max = jnp.max(scores, axis=2, keepdims=True)
        weights = jnp.exp(scores - row_max)
        row_sum = jnp.sum(weights, axis=2, keepdims=True)
        probs_low = (weights / row_sum).astype(jnp.bfloat16)
        result = jnp.einsum(
            "hqk,khd->qhd", probs_low, values_near, preferred_element_type=jnp.float32
        )
        result = result * keep_block[:, None, None].astype(jnp.float32)
        return (result.astype(jnp.bfloat16), row_max, row_sum)

    block_ids = jnp.arange(block_count, dtype=jnp.int32)
    blocked = (
        query_heads.reshape(block_count, QBLOCK, local_heads, HEAD_DIM),
        seg_all.reshape(block_count, QBLOCK),
        keep_all.reshape(block_count, QBLOCK),
        block_ids,
    )
    results, block_max, block_sums = lax.map(one_block, blocked)
    return (results.reshape(all_rows, local_heads * HEAD_DIM), block_max, block_sums)


def attention_backward(head_rows, grad_rows, seg_all, keep_all, block_max, block_sums):
    all_rows = head_rows.shape[0]
    block_count = all_rows // QBLOCK
    window = key_window(all_rows)
    query_heads, key_heads, value_heads = split_heads(head_rows)
    local_heads = query_heads.shape[1]
    score_scale = HEAD_DIM ** (-0.5)

    def one_block(running, block_parts):
        grad_keys, grad_values = running
        query_block, seg_block, keep_block, grad_block, row_max, row_sum, block_index = block_parts
        start = window_start(block_index, all_rows, window)
        keys_near = lax.dynamic_slice_in_dim(key_heads, start, window, 0)
        values_near = lax.dynamic_slice_in_dim(value_heads, start, window, 0)
        seg_near = lax.dynamic_slice_in_dim(seg_all, start, window, 0)
        keep_near = lax.dynamic_slice_in_dim(keep_all, start, window, 0)
        scores = block_scores(query_block, keys_near, seg_block, seg_near, keep_near)
        probs = jnp.exp(scores - row_max) / row_sum
        grad_result = grad_block * keep_block[:, None, None].astype(jnp.bfloat16)
        values_term = jnp.einsum(
            "hqk,qhd->khd",
            probs.astype(jnp.bfloat16),
            grad_result,
            preferred_element_type=jnp.float32,
        )
        grad_probs = jnp.einsum(
            "qhd,khd->hqk", grad_result, values_near, preferred_element_type=jnp.float32
        )
        row_inner = jnp.sum(probs * grad_probs, axis=2, keepdims=True)
        grad_scores = (probs * (grad_probs - row_inner)).astype(jnp.bfloat16)
        grad_query = (
            jnp.einsum("hqk,khd->qhd", grad_scores, keys_near, preferred_element_type=jnp.float32)
            * score_scale
        )
        keys_term = (
            jnp.einsum("hqk,qhd->khd", grad_scores, query_block, preferred_element_type=jnp.float32)
            * score_scale
        )
        grad_keys = lax.dynamic_update_slice_in_dim(
            grad_keys, lax.dynamic_slice_in_dim(grad_keys, start, window, 0) + keys_term, start, 0
        )
        grad_values = lax.dynamic_update_slice_in_dim(
            grad_values,
            lax.dynamic_slice_in_dim(grad_values, start, window, 0) + values_term,
            start,
            0,
        )
        return ((grad_keys, grad_values), grad_query)

    zero_heads = jnp.zeros((all_rows, local_heads, HEAD_DIM), jnp.float32)
    block_ids = jnp.arange(block_count, dtype=jnp.int32)
    blocked = (
        query_heads.reshape(block_count, QBLOCK, local_heads, HEAD_DIM),
        seg_all.reshape(block_count, QBLOCK),
        keep_all.reshape(block_count, QBLOCK),
        grad_rows.reshape(block_count, QBLOCK, local_heads, HEAD_DIM),
        block_max,
        block_sums,
        block_ids,
    )
    (grad_keys, grad_values), grad_queries = lax.scan(one_block, (zero_heads, zero_heads), blocked)
    flat_width = local_heads * HEAD_DIM
    stacked = jnp.stack(
        [
            grad_queries.reshape(all_rows, flat_width),
            grad_keys.reshape(all_rows, flat_width),
            grad_values.reshape(all_rows, flat_width),
        ],
        axis=1,
    )
    return stacked.astype(jnp.bfloat16)


def per_device(
    tokens,
    grad_out,
    segments,
    padding,
    adapter_ids,
    norm1_gain,
    norm1_bias,
    w_qkv,
    w_proj,
    proj_bias,
    norm2_gain,
    norm2_bias,
    w_fc1,
    fc1_bias,
    w_fc2,
    fc2_bias,
    qkv_down,
    qkv_up,
    proj_down,
    proj_up,
    fc1_down,
    fc1_up,
    fc2_down,
    fc2_up,
):
    tok_rows = tokens.shape[1]
    feat_width = tokens.shape[2]
    inputs = tokens[0].astype(jnp.float32)
    seg_all = segments[0]
    keep_all = padding[0]
    offset = lax.axis_index("seq") * tok_rows
    seg_own = lax.dynamic_slice_in_dim(seg_all, offset, tok_rows)
    select = selection(seg_own, adapter_ids[0], qkv_down.shape[1])
    gain_one, shift_one, qkv_weight, proj_weight, proj_shift = (
        lax.all_gather(norm1_gain, "fsdp", axis=0, tiled=True),
        lax.all_gather(norm1_bias, "fsdp", axis=0, tiled=True),
        lax.all_gather(w_qkv, "fsdp", axis=0, tiled=True),
        lax.all_gather(w_proj, "fsdp", axis=0, tiled=True),
        lax.all_gather(proj_bias, "fsdp", axis=0, tiled=True),
    )
    gain_one = gain_one.astype(jnp.float32)
    shift_one = shift_one.astype(jnp.float32)
    normed_one = layer_norm(inputs, gain_one, shift_one).astype(jnp.bfloat16)
    qkv_main, inner_one = adapter_forward(normed_one, qkv_weight, qkv_down, qkv_up, select)
    qkv_low = qkv_main.astype(jnp.bfloat16).reshape(tok_rows, 3, feat_width)
    head_rows = lax.all_to_all(qkv_low, "seq", split_axis=2, concat_axis=0, tiled=True)
    attended_heads, block_max, block_sums = attention_forward(head_rows, seg_all, keep_all)
    attended = lax.all_to_all(attended_heads, "seq", split_axis=0, concat_axis=1, tiled=True)
    branch_one, inner_two = adapter_forward(attended, proj_weight, proj_down, proj_up, select)
    middle = inputs + (branch_one + proj_shift.astype(jnp.float32))
    gain_two, shift_two, fc1_weight, fc2_shift, fc2_weight, fc1_shift = (
        lax.all_gather(norm2_gain, "fsdp", axis=0, tiled=True),
        lax.all_gather(norm2_bias, "fsdp", axis=0, tiled=True),
        lax.all_gather(w_fc1, "fsdp", axis=0, tiled=True),
        lax.all_gather(fc2_bias, "fsdp", axis=0, tiled=True),
        lax.all_gather(w_fc2, "fsdp", axis=0, tiled=True),
        lax.all_gather(fc1_bias, "fsdp", axis=0, tiled=True),
    )
    gain_two = gain_two.astype(jnp.float32)
    shift_two = shift_two.astype(jnp.float32)
    normed_two = layer_norm(middle, gain_two, shift_two).astype(jnp.bfloat16)
    hidden_main, inner_three = adapter_forward(normed_two, fc1_weight, fc1_down, fc1_up, select)
    hidden = hidden_main + fc1_shift.astype(jnp.float32)
    active = jax.nn.gelu(hidden, approximate=False).astype(jnp.bfloat16)
    branch_two, inner_four = adapter_forward(active, fc2_weight, fc2_down, fc2_up, select)
    output = (middle + (branch_two + fc2_shift.astype(jnp.float32))).astype(jnp.bfloat16)
    fc1_back, fc2_back = (
        lax.all_gather(w_fc1, "fsdp", axis=0, tiled=True),
        lax.all_gather(w_fc2, "fsdp", axis=0, tiled=True),
    )
    grad_top = grad_out[0]
    grad_active, grad_fc2_down, grad_fc2_up = adapter_backward(
        active, inner_four, grad_top, fc2_back, fc2_down, fc2_up, select
    )
    unused, gelu_back = jax.vjp(partial(jax.nn.gelu, approximate=False), hidden)
    grad_hidden = gelu_back(grad_active)[0].astype(jnp.bfloat16)
    grad_normed_two, grad_fc1_down, grad_fc1_up = adapter_backward(
        normed_two, inner_three, grad_hidden, fc1_back, fc1_down, fc1_up, select
    )
    grad_middle = grad_top.astype(jnp.float32) + norm_backward(
        middle, gain_two, shift_two, grad_normed_two
    )
    qkv_back, proj_back = (
        lax.all_gather(w_qkv, "fsdp", axis=0, tiled=True),
        lax.all_gather(w_proj, "fsdp", axis=0, tiled=True),
    )
    grad_branch_one = grad_middle.astype(jnp.bfloat16)
    grad_attended, grad_proj_down, grad_proj_up = adapter_backward(
        attended, inner_two, grad_branch_one, proj_back, proj_down, proj_up, select
    )
    grad_head_rows = lax.all_to_all(
        grad_attended.astype(jnp.bfloat16), "seq", split_axis=1, concat_axis=0, tiled=True
    )
    grad_qkv_heads = attention_backward(
        head_rows, grad_head_rows, seg_all, keep_all, block_max, block_sums
    )
    grad_qkv = lax.all_to_all(
        grad_qkv_heads, "seq", split_axis=0, concat_axis=2, tiled=True
    ).reshape(tok_rows, 3 * feat_width)
    grad_normed_one, grad_qkv_down, grad_qkv_up = adapter_backward(
        normed_one, inner_one, grad_qkv, qkv_back, qkv_down, qkv_up, select
    )
    grad_tokens = grad_middle + norm_backward(inputs, gain_one, shift_one, grad_normed_one)
    summed = lax.psum(
        (
            grad_qkv_down,
            grad_qkv_up,
            grad_proj_down,
            grad_proj_up,
            grad_fc1_down,
            grad_fc1_up,
            grad_fc2_down,
            grad_fc2_up,
        ),
        ("seq", "fsdp"),
    )
    return (
        output[None],
        grad_tokens[None],
        summed[0],
        summed[1],
        summed[2],
        summed[3],
        summed[4],
        summed[5],
        summed[6],
        summed[7],
    )


F32 = jnp.float32
BF16 = jnp.bfloat16
MESH = pl.DeviceIdType.MESH
VMEM_LIMIT = 64 * 1000 * 1000


def mm(a, b):
    return lax.dot_general(a, b, (((1,), (0,)), ((), ())), preferred_element_type=F32)


def mm_nt(a, b):
    return lax.dot_general(a, b, (((1,), (1,)), ((), ())), preferred_element_type=F32)


def mm_tn(a, b):
    return lax.dot_general(a, b, (((0,), (0,)), ((), ())), preferred_element_type=F32)


def norm_parts(v):
    mean = jnp.mean(v, axis=-1, keepdims=True)
    centred = v - mean
    r = lax.rsqrt(jnp.mean(centred * centred, axis=-1, keepdims=True) + norm_eps)
    return centred * r, r


def norm_grad(v, gain, grad_y):
    h, r = norm_parts(v)
    d = grad_y * gain
    return r * (d - jnp.mean(d, axis=-1, keepdims=True) - h * jnp.mean(d * h, axis=-1, keepdims=True))


class Net:
    def __init__(self):
        self.s = lax.axis_index("seq")
        self.f = lax.axis_index("fsdp")
        self.z = self.f // 4
        self.x = (self.f // 2) % 2
        self.c = self.f % 2
        self.partner = {"seq": 1 - self.s}
        self.x_peer = {"fsdp": self.block(self.z, 1 - self.x, self.c)}
        self.c_peer = {"fsdp": self.block(self.z, self.x, 1 - self.c)}

    def block(self, z, x, c):
        return (z * 2 + x) * 2 + c

    def z_peer(self, d):
        return {"fsdp": self.block((self.z + d) % 4, self.x, self.c)}

    def barrier(self):
        sem = pltpu.get_barrier_semaphore()
        peers = [self.partner, self.x_peer, self.c_peer] + [self.z_peer(d) for d in (1, 2, 3)]
        for peer in peers:
            pl.semaphore_signal(sem, inc=1, device_id=peer, device_id_type=MESH)
        pl.semaphore_wait(sem, len(peers))


class Block:
    def __init__(self, src, piece, send_sem, recv_sem, own_sem, plane=None):
        self.src, self.piece, self.plane = src, piece, plane
        self.send_sem, self.recv_sem, self.own_sem = send_sem, recv_sem, own_sem


class Gather:
    def __init__(self, net):
        self.net = net

    def copy(self, it, src, block, k, peer):
        return pltpu.make_async_remote_copy(
            src_ref=src, dst_ref=it.piece(block), send_sem=it.send_sem(k), recv_sem=it.recv_sem(block),
            device_id=peer, device_id_type=MESH)

    def arrive(self, it, block):
        piece = it.piece(block)
        self.copy(it, piece, block, 0, self.net.c_peer).wait_recv()
        return piece

    def here(self, it, body):
        if it.plane is None:
            body()
        else:
            pl.when(self.net.s == it.plane)(body)

    def own(self, it):
        return pltpu.make_async_copy(it.src, it.piece(self.net.f), it.own_sem)

    def start(self, it):
        net = self.net

        def along():
            for d in (2, 1, 3):
                self.copy(it, it.src, net.f, d - 1, net.z_peer(d)).start()
            self.copy(it, it.src, net.f, 3, net.x_peer).start()

        self.here(it, along)
        self.copy(it, it.src, net.f, 4, net.c_peer).start()
        self.own(it).start()

    def from_z(self, it):
        net = self.net

        def body():
            for n, d in enumerate((1, 3, 2)):
                block = net.block((net.z + d) % 4, net.x, net.c)
                piece = self.arrive(it, block)
                self.copy(it, piece, block, 5 + 2 * n, net.x_peer).start()
                if it.plane is not None:
                    self.copy(it, piece, block, 15 + n, net.partner).start()
                self.copy(it, piece, block, 6 + 2 * n, net.c_peer).start()

        self.here(it, body)

    def from_x(self, it):
        net = self.net

        def body():
            for n, d in enumerate((0, 1, 3, 2)):
                block = net.block((net.z + d) % 4, 1 - net.x, net.c)
                piece = self.arrive(it, block)
                if it.plane is not None:
                    self.copy(it, piece, block, 18 + n, net.partner).start()
                self.copy(it, piece, block, 11 + n, net.c_peer).start()

        self.here(it, body)

    def from_seq(self, it):
        net = self.net
        if it.plane is None:
            return

        @pl.when(net.s != it.plane)
        def _():
            for n, (d, x) in enumerate(((1, net.x), (3, net.x), (2, net.x), (0, 1 - net.x), (1, 1 - net.x),
                                        (3, 1 - net.x), (2, 1 - net.x))):
                block = net.block((net.z + d) % 4, x, net.c)
                piece = self.arrive(it, block)
                self.copy(it, piece, block, 5 + n, net.c_peer).start()

    def from_core(self, it):
        net = self.net

        @pl.loop(0, 8)
        def _(n):
            self.arrive(it, 2 * n + 1 - net.c)

        self.own(it).wait()

    def finish(self, it):
        net = self.net

        def sent(first, end):
            @pl.loop(first, end)
            def _(k):
                self.copy(it, it.src, net.f, k, net.c_peer).wait_send()

        if it.plane is None:
            sent(0, 15)
            return

        @pl.when(net.s == it.plane)
        def _():
            sent(0, 22)

        @pl.when(net.s != it.plane)
        def _():
            sent(4, 12)


def full_vector(vec_ref, row, blocks=16, rows=16):
    parts = []
    for k in range(blocks // 2):
        even = vec_ref[2 * k * rows + row:2 * k * rows + row + 1, :]
        odd = vec_ref[(2 * k + 1) * rows + row:(2 * k + 1) * rows + row + 1, :]
        parts.append(even + odd)
    return jnp.concatenate(parts, axis=1)


WINDOW = 640
STEP = 64
PAD = 384
QROWS = 320
FFB = 512


class Image:
    def __init__(self, seg_ref, id_ref):
        self.start = jnp.sum((seg_ref[...] == 0).astype(F32), axis=1, keepdims=True)
        ident = id_ref[...].astype(F32)
        self.pick = []
        base = jnp.zeros((1, 1), F32)
        for k in range(PAD // STEP + 1):
            mark = ((self.start >= k * STEP) & (self.start < (k + 1) * STEP)).astype(F32)
            self.pick.append(mark)
            base = base + mark * float(k * STEP)
        self.shift = base - self.start
        lane = lax.broadcasted_iota(jnp.int32, (1, 128), 1).astype(F32)
        self.columns = ((lane >= ident * RANK) & (lane < (ident + 1) * RANK)).astype(F32)

    def choose(self, load):
        total = None
        for k, mark in enumerate(self.pick):
            value = load(k * STEP)
            value = value * mark.astype(value.dtype)
            total = value if total is None else total + value
        return total

    def inside(self, shape, axis, first=0):
        at = (lax.broadcasted_iota(jnp.int32, shape, axis) + first).astype(F32) + self.shift
        return (at >= 0) & (at < IMG)

    def select(self, first, rows):
        at = (lax.broadcasted_iota(jnp.int32, (rows, 1), 0) + first).astype(F32)
        return (at >= self.start).astype(F32) * self.columns

    def select_window(self, first, rows):
        at = (lax.broadcasted_iota(jnp.int32, (rows, 1), 0) + first).astype(F32) + self.shift
        return (at >= 0).astype(F32) * self.columns


def lane_halves():
    lane = lax.broadcasted_iota(jnp.int32, (1, 128), 1)
    return [(lane < 64).astype(F32), (lane >= 64).astype(F32)]


def compact_rows(dense):
    total = dense[0:16]
    for k in range(1, 8):
        total = total + dense[16 * k:16 * (k + 1)]
    return total.astype(BF16)


N_FC1 = 8
N_FC2 = 4
N_ITEMS = 3 + N_FC2 + N_FC1


def forward_kernel(seg_ref, id_ref, x_ref, vec_ref, qd_ref, pd_ref, pu_ref, wq_hbm, wp_hbm, w1_hbm, w2_hbm,
                   qu_hbm, g_hbm, u1_hbm, d1_hbm, u2_hbm, d2_hbm,
                   wqf, wpf, vecf_out, qkv_out, n1_out, c1_out, prob_out, oh_out, att_out, c2_out, gm_out, gr_out, out_out,
                   wq_own, wq, wp, w1, w2, xp, vecf, qu, g, u1, d1, u2, d2, qkv, n1, c1, qkvw, n1w, c1w, prob, opad, sendb,
                   oh, att, c2, mid, n2, oacc, gacc, u4, e3, c3, e4, c3t, e4t, act_s, gh_s, gr,
                   xs_sem, xr_sem, as_sem, ar_sem, loc_sem, out_sem, prob_sem, g_send, g_recv, g_own):
    net = Net()
    s, other = net.s, 1 - net.s
    rows, width = x_ref.shape
    half = wq.shape[1] // 3
    rb = wq_own.shape[0]
    fr1 = w1_hbm.shape[0]
    fr2 = w2_hbm.shape[0]
    ff = w1.shape[1]
    chunk = rows // 2

    pre = []
    for part in range(3):
        cols = pl.ds(pl.multiple_of(part * width + s * half, 128), half)
        pre.append(pltpu.make_async_copy(wq_hbm.at[:, cols], wq_own.at[:, pl.ds(part * half, half)], loc_sem.at[part]))
    late = []
    for part in range(3):
        cols = pl.ds(pl.multiple_of(part * width + s * half, 128), half)
        late.append(pltpu.make_async_copy(qu_hbm.at[:, cols], qu.at[:, pl.ds(part * half, half)], loc_sem.at[3 + part]))
    for n, (src, dst) in enumerate(((g_hbm, g), (u1_hbm, u1), (d1_hbm, d1), (u2_hbm, u2), (d2_hbm, d2))):
        late.append(pltpu.make_async_copy(src, dst, loc_sem.at[6 + n]))
    for copy in pre + late:
        copy.start()
    net.barrier()

    def x_copy(i):
        part = pl.ds(i * chunk, chunk)
        return pltpu.make_async_remote_copy(
            src_ref=x_ref.at[part, :], dst_ref=xp.at[part, :], send_sem=xs_sem.at[i], recv_sem=xr_sem.at[i],
            device_id=net.partner, device_id_type=MESH)

    for i in range(2):
        x_copy(i).start()
    for copy in pre:
        copy.wait()

    def block(n, src, piece, plane=None):
        return Block(src, piece, lambda k: g_send.at[n, k], lambda b: g_recv.at[n, b], g_own.at[n], plane)

    sub = fr2 // N_FC2
    vec_it = block(0, vec_ref, lambda b: vecf.at[pl.ds(b * 16, 16), :])
    wq_it = block(1, wq_own, lambda b: wq.at[pl.ds(b * rb, rb), :])
    wp_it = block(2, wp_hbm, lambda b: wp.at[pl.ds(b * rb, rb), :])
    fc2_it = [block(3 + j, w2_hbm.at[pl.ds(j * sub, sub), :], lambda b, j=j: w2.at[pl.ds(b * fr2 + j * sub, sub), :],
                    (0, 1, None, None)[j]) for j in range(N_FC2)]

    def fc1_it(j):
        cols = pl.ds(j * FFB if isinstance(j, int) else pl.multiple_of(j * FFB, FFB), FFB)
        return block(3 + N_FC2 + j, w1_hbm.at[:, cols], lambda b: w1.at[pl.ds(b * fr1, fr1), cols], j % 2)

    gather = Gather(net)
    gather.start(vec_it)
    gather.start(wq_it)
    image = Image(seg_ref, id_ref)
    zeros = jnp.zeros((PAD, 128), BF16)
    opad[0:PAD, :] = zeros
    opad[PAD + WINDOW:2 * PAD + WINDOW, :] = zeros
    gather.from_z(vec_it)
    gather.from_z(wq_it)
    gather.start(wp_it)
    gather.from_x(vec_it)
    gather.from_x(wq_it)
    gather.start(fc2_it[0])
    gather.start(fc2_it[1])
    for copy in late:
        copy.wait()
    gather.from_core(vec_it)
    gather.from_core(wq_it)

    gain1 = full_vector(vecf, 0)
    shift1 = full_vector(vecf, 1)

    def project(src, src_row, row):
        v = src[pl.ds(src_row, chunk), :].astype(F32)
        h, unused = norm_parts(v)
        normed = (h * gain1 + shift1).astype(BF16)
        at = pl.ds(row, chunk)
        n1[at, :] = normed
        inner = (mm(normed, qd_ref[...]) * image.select(row, chunk)).astype(BF16)
        c1[at, :] = inner
        for part in range(3):
            cols = pl.ds(part * half, half)
            qkv[at, cols] = (mm(normed, wq[:, cols]) + mm(inner, qu[:, cols])).astype(BF16)

    @pl.loop(0, 2)
    def _(i):
        project(x_ref, pl.multiple_of(i * chunk, chunk), pl.multiple_of(s * rows + i * chunk, chunk))

    gather.from_z(wp_it)
    gather.start(fc2_it[2])

    @pl.loop(0, 2)
    def _(i):
        pltpu.make_async_remote_copy(
            src_ref=x_ref.at[pl.ds(0, chunk), :], dst_ref=xp.at[pl.ds(0, chunk), :], send_sem=xs_sem.at[i],
            recv_sem=xr_sem.at[i], device_id=net.partner, device_id_type=MESH).wait_recv()
        project(xp, pl.multiple_of(i * chunk, chunk), pl.multiple_of(other * rows + i * chunk, chunk))

    gather.from_x(wp_it)
    gather.from_z(fc2_it[0])
    gather.from_z(fc2_it[1])
    outs = []

    def put(src, dst):
        copy = pltpu.make_async_copy(src, dst, out_sem.at[len(outs)])
        copy.start()
        outs.append(copy)

    put(wq, wqf)
    put(vecf, vecf_out)
    for src, dst in ((qkv, qkvw), (n1, n1w), (c1, c1w)):
        step = min(src.shape[1], 512)

        @pl.loop(0, src.shape[1] // step)
        def _(n, src=src, dst=dst, step=step):
            cols = pl.ds(pl.multiple_of(n * step, step), step)
            dst[:, cols] = image.choose(lambda at: src[at:at + WINDOW, cols])
    put(qkvw, qkv_out)
    put(n1w, n1_out)
    put(c1w, c1_out)
    bias = jnp.where(image.inside((1, WINDOW), 1), 0.0, masked_score).astype(F32)
    halves = lane_halves()

    def prob_copy(pair):
        slot = lax.rem(pair, 2)
        return pltpu.make_async_copy(prob.at[slot], prob_out.at[pl.ds(2 * pair, 2)], prob_sem.at[slot])

    def att_copy(pair):
        cols = pl.ds(pl.multiple_of(s * half + pair * 128, 128), 128)
        return pltpu.make_async_remote_copy(
            src_ref=sendb.at[pair], dst_ref=att.at[:, cols], send_sem=as_sem.at[pair], recv_sem=ar_sem.at[pair],
            device_id=net.partner, device_id_type=MESH)

    pairs = half // 128

    @pl.loop(0, pairs)
    def _(pair):
        def cols(part):
            return pl.ds(pl.multiple_of(part * half + pair * 128, 128), 128)

        k2 = qkvw[:, cols(1)]
        v2 = qkvw[:, cols(2)]
        vs = [(v2 * hm.astype(BF16)) for hm in halves]
        slot = lax.rem(pair, 2)

        @pl.when(pair >= 2)
        def _():
            prob_copy(pair).wait()

        @pl.loop(0, WINDOW // QROWS)
        def _(b):
            r0 = pl.multiple_of(b * QROWS, QROWS)
            q2 = qkvw[pl.ds(r0, QROWS), cols(0)]
            q2 = q2 * jnp.asarray(HEAD_DIM ** (-0.5), BF16)
            total = None
            for hd in range(2):
                scores = mm_nt(q2 * halves[hd].astype(BF16), k2) + bias
                weights = jnp.exp(scores - jnp.max(scores, axis=1, keepdims=True))
                weights = (weights * (1.0 / jnp.sum(weights, axis=1, keepdims=True))).astype(BF16)
                prob[slot, hd, pl.ds(r0, QROWS), :] = weights
                part = mm(weights, vs[hd])
                total = part if total is None else total + part
            total = (total * image.inside((QROWS, 1), 0, r0).astype(F32)).astype(BF16)
            opad[pl.ds(PAD + r0, QROWS), :] = total
            oh[pl.ds(r0, QROWS), cols(0)] = total

        prob_copy(pair).start()

        def own_rows(who):
            return image.choose(lambda at: opad[pl.ds(pl.multiple_of(who * rows + PAD - at, STEP), rows), :])

        sendb[pair] = own_rows(other)
        att_copy(pair).start()
        att[:, pl.ds(pl.multiple_of(s * half + pair * 128, 128), 128)] = own_rows(s)

        @pl.when(pair == 0)
        def _():
            gather.from_core(wp_it)
            gather.from_x(fc2_it[0])
            gather.from_x(fc2_it[1])

        @pl.when(pair == 1)
        def _():
            gather.start(fc2_it[3])
            gather.from_z(fc2_it[2])

        @pl.when(pair == 2)
        def _():
            gather.from_seq(fc2_it[0])
            gather.from_seq(fc2_it[1])
            gather.start(fc1_it(0))
            gather.start(fc1_it(1))

        @pl.when(pair == 3)
        def _():
            gather.from_x(fc2_it[2])
            gather.from_z(fc2_it[3])

    put(wp, wpf)
    put(oh, oh_out)

    @pl.loop(0, pairs)
    def _(pair):
        att_copy(pair).wait_recv()

    put(att, att_out)
    bias_p = full_vector(vecf, 2)
    gain2 = full_vector(vecf, 3)
    shift2 = full_vector(vecf, 4)

    @pl.loop(0, 2)
    def _(i):
        at = pl.ds(pl.multiple_of(i * chunk, chunk), chunk)
        rows_in = att[at, :]
        own_select = image.select(s * rows + i * chunk, chunk)
        inner = (mm(rows_in, pd_ref[...]) * own_select).astype(BF16)
        c2[at, :] = inner
        branch = mm(rows_in, wp[...]) + mm(inner, pu_ref[...]) + bias_p
        middle = x_ref[at, :].astype(F32) + branch
        mid[at, :] = middle
        h, unused = norm_parts(middle)
        normed = (h * gain2 + shift2).astype(BF16)
        n2[at, :] = normed
        c = mm(normed, d1[...]) * own_select
        e = mm_nt(g[at, :], u2[...]) * own_select
        c3[at, :] = c.astype(BF16)
        e4[at, :] = e.astype(BF16)
        oacc[at, :] = jnp.zeros((chunk, width), F32)
        gacc[at, :] = jnp.zeros((chunk, width), F32)
        u4[at, :] = jnp.zeros((chunk, 128), F32)
        e3[at, :] = jnp.zeros((chunk, 128), F32)

    c3t[...] = c3[...].T
    e4t[...] = e4[...].T
    put(c2, c2_out)
    gather.start(fc1_it(2))
    gather.from_z(fc1_it(0))
    gather.from_z(fc1_it(1))
    gather.from_x(fc2_it[3])
    gather.start(fc1_it(3))
    gather.from_x(fc1_it(0))
    gather.from_x(fc1_it(1))
    gather.from_z(fc1_it(2))
    gather.start(fc1_it(4))
    for j in range(N_FC2):
        gather.from_core(fc2_it[j])
    gather.from_seq(fc1_it(0))

    @pl.loop(0, N_FC1)
    def _(j):
        @pl.when(j + 5 < N_FC1)
        def _():
            gather.start(fc1_it(j + 5))

        @pl.when(j + 3 < N_FC1)
        def _():
            gather.from_z(fc1_it(j + 3))

        @pl.when(j + 2 < N_FC1)
        def _():
            gather.from_x(fc1_it(j + 2))

        @pl.when(j + 1 < N_FC1)
        def _():
            gather.from_seq(fc1_it(j + 1))

        gather.from_core(fc1_it(j))
        bias = jnp.concatenate([vecf[pl.ds(2 * j * 16 + 6, 1), :], vecf[pl.ds(2 * j * 16 + 7, 1), :],
                                vecf[pl.ds((2 * j + 1) * 16 + 6, 1), :], vecf[pl.ds((2 * j + 1) * 16 + 7, 1), :]], axis=1)
        col = pl.ds(pl.multiple_of(j * FFB, FFB), FFB)

        @pl.loop(0, 2)
        def _(i):
            at = pl.ds(pl.multiple_of(i * chunk, chunk), chunk)
            hidden = mm(n2[at, :], w1[:, col]) + mm(c3[at, :], u1[:, col]) + bias
            cdf = 0.5 * (1.0 + lax.erf(hidden * (0.5 ** 0.5)))
            pdf = jnp.exp(hidden * hidden * -0.5) * (0.5 / 3.141592653589793) ** 0.5
            active = (hidden * cdf).astype(BF16)
            act_s[at, :] = active
            grad_active = mm_nt(g[at, :], w2[col, :]) + mm_nt(e4[at, :], d2[col, :])
            grad_hidden = (grad_active * (cdf + hidden * pdf)).astype(BF16)
            gh_s[at, :] = grad_hidden
            oacc[at, :] += mm(active, w2[col, :])
            u4[at, :] += mm(active, d2[col, :])
            gacc[at, :] += mm_nt(grad_hidden, w1[:, col])
            e3[at, :] += mm_nt(grad_hidden, u1[:, col])

        gr[:, col] = compact_rows(mm(c3t[...], gh_s[...]))
        gr[:, pl.ds(pl.multiple_of(ff + j * FFB, FFB), FFB)] = compact_rows(mm(e4t[...], act_s[...]))

    bias2 = full_vector(vecf, 5)

    @pl.loop(0, 2)
    def _(i):
        at = pl.ds(pl.multiple_of(i * chunk, chunk), chunk)
        own_select = image.select(s * rows + i * chunk, chunk)
        c = (u4[at, :] * own_select).astype(BF16)
        e = (e3[at, :] * own_select).astype(BF16)
        c3[at, :] = c
        e4[at, :] = e
        act_out = mid[at, :] + (oacc[at, :] + mm(c, u2[...]) + bias2)
        xp[at, :] = act_out.astype(BF16)
        grad_n2 = gacc[at, :] + mm_nt(e, d1[...])
        gacc[at, :] = g[at, :].astype(F32) + norm_grad(mid[at, :], gain2, grad_n2)

    put(xp, out_out)
    put(gacc, gm_out)
    gr[:, 2 * ff:2 * ff + width] = compact_rows(mm_tn(e4[...], n2[...]))
    gr[:, 2 * ff + width:2 * ff + 2 * width] = compact_rows(mm_tn(c3[...], g[...]))
    put(gr, gr_out)
    for copy in outs:
        copy.wait()
    for pair in range(pairs - 2, pairs):
        prob_copy(pair).wait()
    for i in range(2):
        x_copy(i).wait_send()

    @pl.loop(0, pairs)
    def _(pair):
        att_copy(pair).wait_send()

    for it in [vec_it, wq_it, wp_it] + fc2_it:
        gather.finish(it)

    @pl.loop(0, N_FC1)
    def _(j):
        gather.finish(fc1_it(j))


def any_spec():
    return pl.BlockSpec(memory_space=pl.ANY)


def vmem_spec():
    return pl.BlockSpec(memory_space=pltpu.VMEM)


def run_forward(seg, ident, x, vec, qd, pd, pu, wq, wp, w1, w2, qu, g, u1, d1, u2, d2):
    rows, width = x.shape
    toks = seg.shape[1]
    half = width // 2
    ff = w1.shape[1]
    dma = pltpu.SemaphoreType.DMA
    sds = jax.ShapeDtypeStruct
    gcols = 2 * ff + 2 * width
    out_shape = (
        sds((width, 3 * half), BF16), sds((width, width), BF16), sds((256, 128), F32),
        sds((WINDOW, 3 * half), BF16), sds((WINDOW, width), BF16), sds((WINDOW, 128), BF16),
        sds((half // 64, WINDOW, WINDOW), BF16), sds((WINDOW, half), BF16), sds((rows, width), BF16), sds((rows, 128), BF16),
        sds((rows, width), F32), sds((16, gcols), BF16), sds((rows, width), BF16))

    def low(*shape):
        return pltpu.VMEM(shape, BF16)

    def full(*shape):
        return pltpu.VMEM(shape, F32)

    scratch = [
        low(wq.shape[0], 3 * half), low(width, 3 * half), low(width, width), low(width, ff), low(ff, width),
        low(rows, width), full(256, 128), low(128, 3 * half), low(rows, width), low(128, ff), low(width, 128),
        low(128, width), low(ff, 128), low(toks, 3 * half), low(toks, width), low(toks, 128),
        low(WINDOW, 3 * half), low(WINDOW, width), low(WINDOW, 128), low(2, 2, WINDOW, WINDOW), low(2 * PAD + WINDOW, 128),
        low(half // 128, rows, 128), low(WINDOW, half), low(rows, width), low(rows, 128), full(rows, width), low(rows, width),
        full(rows, width), full(rows, width), full(rows, 128), full(rows, 128), low(rows, 128), low(rows, 128),
        low(128, rows), low(128, rows), low(rows, FFB), low(rows, FFB), low(16, gcols),
        dma((2,)), dma((2,)), dma((4,)), dma((4,)), dma((11,)), dma((12,)), dma((2,)),
        dma((N_ITEMS, 22)), dma((N_ITEMS, 16)), dma((N_ITEMS,))]
    return pl.pallas_call(
        forward_kernel, out_shape=out_shape, in_specs=[vmem_spec()] * 7 + [any_spec()] * 10,
        out_specs=tuple(any_spec() for unused in out_shape), scratch_shapes=scratch,
        compiler_params=pltpu.CompilerParams(collective_id=1, has_side_effects=True, vmem_limit_bytes=VMEM_LIMIT),
        name="forward")(seg, ident, x, vec, qd, pd, pu, wq, wp, w1, w2, qu, g, u1, d1, u2, d2)


def backward_kernel(seg_ref, id_ref, gm_ref, att_ref, c2_ref, oh_ref, pd_ref, pu_ref, qd_ref, gf_ref, wp_ref,
                    wq_hbm, qkv_hbm, n1_hbm, c1_hbm, prob_hbm, qu_hbm,
                    gall, gn_out,
                    wq, qkv, n1, c1, prob, qu, g1, e2, gsend, do_s, first_own, first_send, first_in, gq, qsend, qdown, qdown_in, qown,
                    gpad, psend, prcv, gn,
                    loc_sem, ds_sem, dr_sem, fs_sem, fr_sem, qs_sem, qr_sem, ps_sem, pr_sem, out_sem, g_send, g_recv, g_own):
    net = Net()
    s, other = net.s, 1 - net.s
    image = Image(seg_ref, id_ref)
    rows, width = gm_ref.shape
    half = wq.shape[1] // 3
    chunk = rows // 2
    ffn_cols = gf_ref.shape[1]

    loads = [pltpu.make_async_copy(src, dst, loc_sem.at[i]) for i, (src, dst) in enumerate(
        [(qkv_hbm, qkv), (prob_hbm, prob), (wq_hbm, wq), (n1_hbm, n1), (c1_hbm, c1)])]
    for part in range(3):
        cols = pl.ds(pl.multiple_of(part * width + s * half, 128), half)
        loads.append(pltpu.make_async_copy(qu_hbm.at[:, cols], qu.at[:, pl.ds(part * half, half)], loc_sem.at[5 + part]))
    for copy in loads:
        copy.start()
    net.barrier()

    @pl.loop(0, 2)
    def _(i):
        at = pl.ds(pl.multiple_of(i * chunk, chunk), chunk)
        low = gm_ref[at, :].astype(BF16)
        g1[at, :] = low
        e2[at, :] = mm_nt(low, pu_ref[...]) * image.select(s * rows + i * chunk, chunk)

    def grad_att(i, who):
        at = pl.ds(i * chunk, chunk)
        heads = pl.ds(pl.multiple_of(who * half, half), half)
        return (mm_nt(g1[at, :], wp_ref[heads, :]) + mm_nt(e2[at, :].astype(BF16), pd_ref[heads, :])).astype(BF16)

    dsend = []
    for i in range(2):
        gsend[i] = grad_att(i, other)
        copy = pltpu.make_async_remote_copy(
            src_ref=gsend.at[i], dst_ref=do_s.at[pl.ds(pl.multiple_of(s * rows + i * chunk, chunk), chunk), :],
            send_sem=ds_sem.at[i], recv_sem=dr_sem.at[i], device_id=net.partner, device_id_type=MESH)
        copy.start()
        dsend.append(copy)
    first_own[:, 0:ffn_cols] = gf_ref[...]
    first_own[:, ffn_cols:ffn_cols + width] = compact_rows(mm_tn(c2_ref[...], g1[...]))
    first_own[:, ffn_cols + width:ffn_cols + 2 * width] = compact_rows(mm_tn(e2[...].astype(BF16), att_ref[...]))
    fsend = pltpu.make_async_remote_copy(
        src_ref=first_own, dst_ref=first_in, send_sem=fs_sem.at[0], recv_sem=fr_sem.at[0],
        device_id=net.partner, device_id_type=MESH)
    fsend.start()
    for i in range(2):
        do_s[pl.ds(pl.multiple_of(s * rows + i * chunk, chunk), chunk), :] = grad_att(i, s)
    n_first = first_own.shape[1]
    items = [Block(src, lambda b, cols=cols: gall.at[pl.ds(b * 16, 16), cols], lambda k, n=n: g_send.at[n, k],
                   lambda b, n=n: g_recv.at[n, b], g_own.at[n])
             for n, (src, cols) in enumerate(((first_send, pl.ds(0, n_first)), (qown, pl.ds(n_first, 4 * width))))]
    gather = Gather(net)
    zeros = jnp.zeros((PAD, width), F32)
    gpad[0:PAD, :] = zeros
    gpad[PAD + WINDOW:2 * PAD + WINDOW, :] = zeros
    for copy in loads:
        copy.wait()
    for copy in dsend:
        copy.wait_recv()
    fsend.wait_recv()
    first_send[...] = (first_own[...].astype(F32) + first_in[...].astype(F32)).astype(BF16)
    gather.start(items[0])

    halves = lane_halves()
    scale = HEAD_DIM ** (-0.5)
    keep = image.inside((WINDOW, 1), 0).astype(BF16)
    for pair in range(half // 128):
        cols = slice(pair * 128, (pair + 1) * 128)
        k2 = qkv[:, half + pair * 128:half + (pair + 1) * 128]
        v2 = qkv[:, 2 * half + pair * 128:2 * half + (pair + 1) * 128]
        q2 = qkv[:, cols] * jnp.asarray(scale, BF16)
        do2 = image.choose(lambda at: do_s[at:at + WINDOW, cols]) * keep
        inner = do2.astype(F32) * oh_ref[:, cols].astype(F32)
        gv = gk = gqq = None
        for hd in range(2):
            hm = halves[hd].astype(BF16)
            weights = prob[2 * pair + hd]
            grad_p = mm_nt(do2 * hm, v2)
            row_inner = jnp.sum(inner * halves[hd], axis=1, keepdims=True)
            grad_s = (weights.astype(F32) * (grad_p - row_inner)).astype(BF16)
            dv = mm_tn(weights, do2 * hm)
            dk = mm_tn(grad_s, q2 * hm)
            dq = mm(grad_s, k2 * hm)
            gv = dv if gv is None else gv + dv
            gk = dk if gk is None else gk + dk
            gqq = dq if gqq is None else gqq + dq
        gq[:, cols] = (gqq * scale).astype(BF16)
        gq[:, half + pair * 128:half + (pair + 1) * 128] = gk.astype(BF16)
        gq[:, 2 * half + pair * 128:2 * half + (pair + 1) * 128] = gv.astype(BF16)
        if pair == 1:
            gather.from_z(items[0])
        if pair == 2:
            gather.from_x(items[0])

    up = compact_rows(mm_tn(c1[...], gq[...]))
    e1 = (mm_nt(gq[...], qu[...]) * image.select_window(0, WINDOW)).astype(BF16)
    down = mm_tn(e1, n1[...])
    qdown[...] = compact_rows(down)
    qsends = []
    for part in range(3):
        cols = pl.ds(pl.multiple_of(part * width + s * half, 128), half)
        qsend[:, pl.ds(part * half, half)] = up[:, part * half:(part + 1) * half]
        qown[:, cols] = up[:, part * half:(part + 1) * half]
        qsends.append(pltpu.make_async_remote_copy(
            src_ref=qsend.at[:, pl.ds(part * half, half)], dst_ref=qown.at[:, cols], send_sem=qs_sem.at[part],
            recv_sem=qr_sem.at[part], device_id=net.partner, device_id_type=MESH))
    qsends.append(pltpu.make_async_remote_copy(
        src_ref=qdown, dst_ref=qdown_in, send_sem=qs_sem.at[3],
        recv_sem=qr_sem.at[3], device_id=net.partner, device_id_type=MESH))
    for copy in qsends:
        copy.start()

    @pl.loop(0, 2)
    def _(i):
        at = pl.ds(pl.multiple_of(i * QROWS, QROWS), QROWS)
        e1_rows = (mm_nt(gq[at, :], qu[...]) * image.select_window(i * QROWS, QROWS)).astype(BF16)
        gpad[pl.ds(pl.multiple_of(PAD + i * QROWS, STEP), QROWS), :] = mm_nt(gq[at, :], wq[...]) + mm_nt(e1_rows, qd_ref[...])

    psends = []
    for i in range(2):
        psend[i] = image.choose(lambda at: gpad[
            pl.ds(pl.multiple_of(other * rows + PAD + i * chunk - at, STEP), chunk), :]).astype(BF16)
        copy = pltpu.make_async_remote_copy(
            src_ref=psend.at[i], dst_ref=prcv.at[i], send_sem=ps_sem.at[i], recv_sem=pr_sem.at[i],
            device_id=net.partner, device_id_type=MESH)
        copy.start()
        psends.append(copy)
    for copy in qsends:
        copy.wait_recv()
    qown[:, 3 * width:4 * width] = (qdown[...].astype(F32) + qdown_in[...].astype(F32)).astype(BF16)
    gather.start(items[1])
    gather.from_core(items[0])
    gather.from_z(items[1])
    gather.from_x(items[1])
    gather.from_core(items[1])
    outs = []
    for i in range(2):
        psends[i].wait_recv()
        rows_at = pl.ds(i * chunk, chunk)
        gn[rows_at, :] = prcv[i].astype(F32) + image.choose(lambda at: gpad[
            pl.ds(pl.multiple_of(s * rows + PAD + i * chunk - at, STEP), chunk), :])
        copy = pltpu.make_async_copy(gn.at[rows_at, :], gn_out.at[rows_at, :], out_sem.at[i])
        copy.start()
        outs.append(copy)
    for copy in outs:
        copy.wait()
    for copy in dsend + [fsend] + qsends + psends:
        copy.wait_send()
    for it in items:
        gather.finish(it)


def run_backward(seg, ident, gm, att, c2, oh, pd, pu, qd, gf, wp, wq, qkv, n1, c1, prob, qu):
    rows, width = gm.shape
    toks = 2 * rows
    half = width // 2
    dma = pltpu.SemaphoreType.DMA
    sds = jax.ShapeDtypeStruct
    n_first = gf.shape[1] + 2 * width
    out_shape = (sds((256, n_first + 4 * width), BF16), sds((rows, width), F32))
    chunk = rows // 2
    scratch = [
        pltpu.VMEM(wq.shape, BF16), pltpu.VMEM(qkv.shape, BF16), pltpu.VMEM(n1.shape, BF16), pltpu.VMEM(c1.shape, BF16),
        pltpu.VMEM(prob.shape, BF16), pltpu.VMEM((128, 3 * half), BF16), pltpu.VMEM((rows, width), BF16),
        pltpu.VMEM((rows, 128), F32), pltpu.VMEM((2, chunk, half), BF16), pltpu.VMEM((toks, half), BF16),
        pltpu.VMEM((16, n_first), BF16), pltpu.VMEM((16, n_first), BF16), pltpu.VMEM((16, n_first), BF16),
        pltpu.VMEM((WINDOW, 3 * half), BF16), pltpu.VMEM((16, 3 * half), BF16), pltpu.VMEM((16, width), BF16),
        pltpu.VMEM((16, width), BF16), pltpu.VMEM((16, 4 * width), BF16), pltpu.VMEM((2 * PAD + WINDOW, width), F32), pltpu.VMEM((2, chunk, width), BF16),
        pltpu.VMEM((2, chunk, width), BF16), pltpu.VMEM((rows, width), F32),
        dma((8,)), dma((2,)), dma((2,)), dma((1,)), dma((1,)), dma((4,)), dma((4,)), dma((2,)), dma((2,)), dma((2,)),
        dma((2, 15)), dma((2, 16)), dma((2,))]
    return pl.pallas_call(
        backward_kernel, out_shape=out_shape,
        in_specs=[vmem_spec()] * 11 + [any_spec()] * 6,
        out_specs=tuple(any_spec() for unused in out_shape), scratch_shapes=scratch,
        compiler_params=pltpu.CompilerParams(collective_id=2, has_side_effects=True, vmem_limit_bytes=VMEM_LIMIT),
        name="backward")(seg, ident, gm, att, c2, oh, pd, pu, qd, gf, wp, wq, qkv, n1, c1, prob, qu)


def expand_kernel(vec_ref, f1u, f2d, f1d, f2u, pu, pdn, qu, qd, gn, x, gm,
                  gt_out, qd_out, qu_out, pd_out, pu_out, f1d_out, f1u_out, f2d_out, f2u_out):
    ids = jnp.concatenate([jnp.broadcast_to(vec_ref[16 * p + 8:16 * p + 9, :], (16, 128)) for p in range(16)], axis=0)
    r = lax.broadcasted_iota(jnp.int32, (256, 128), 0) % 16
    col = lax.broadcasted_iota(jnp.int32, (256, 128), 1)
    pick = ((ids.astype(jnp.int32) == col // 16) & (r == col % 16)).astype(F32)
    pick_t = pick.T.astype(BF16)
    for src, dst in ((f1u, f1u_out), (f2u, f2u_out), (pu, pu_out), (qu, qu_out)):
        dst[...] = mm(pick_t, src[...])
    for src, dst in ((f1d, f1d_out), (f2d, f2d_out), (pdn, pd_out), (qd, qd_out)):
        dst[...] = mm(pick_t, src[...]).T
    gain1 = full_vector(vec_ref, 0)
    gt_out[...] = gm[...] + norm_grad(x[...].astype(F32), gain1, gn[...])


def run_expand(vec, gall, gn, x, gm):
    rows, width = gn.shape
    ff = 4 * width
    n = 4
    sds = jax.ShapeDtypeStruct

    def part(cols, offset):
        return pl.BlockSpec((256, cols), lambda j: (0, offset // cols + j))

    def by_row(shape):
        return pl.BlockSpec(shape, lambda j: (j, 0))

    def by_col(shape):
        return pl.BlockSpec(shape, lambda j: (0, j))

    q = width // n
    return pl.pallas_call(
        expand_kernel, grid=(n,),
        out_shape=(sds((rows, width), F32), sds((width, 128), F32), sds((128, 3 * width), F32), sds((width, 128), F32),
                   sds((128, width), F32), sds((width, 128), F32), sds((128, ff), F32), sds((ff, 128), F32), sds((128, width), F32)),
        in_specs=[pl.BlockSpec((256, 128), lambda j: (0, 0)), part(ff // n, 0), part(ff // n, ff), part(q, 2 * ff),
                  part(q, 2 * ff + width), part(q, 2 * ff + 2 * width), part(q, 2 * ff + 3 * width),
                  part(3 * q, 2 * ff + 4 * width), part(q, 2 * ff + 7 * width),
                  by_row((rows // n, width)), by_row((rows // n, width)), by_row((rows // n, width))],
        out_specs=(by_row((rows // n, width)), by_row((q, 128)), by_col((128, 3 * q)), by_row((q, 128)), by_col((128, q)),
                   by_row((q, 128)), by_col((128, ff // n)), by_row((ff // n, 128)), by_col((128, q))),
        compiler_params=pltpu.CompilerParams(vmem_limit_bytes=VMEM_LIMIT),
        name="expand")(vec, *([gall] * 8), gn, x, gm)


def per_device_fast(tokens, grad_out, segments, padding, adapter_ids, norm1_gain, norm1_bias, w_qkv, w_proj, proj_bias,
                    norm2_gain, norm2_bias, w_fc1, fc1_bias, w_fc2, fc2_bias, qkv_down, qkv_up, proj_down, proj_up,
                    fc1_down, fc1_up, fc2_down, fc2_up):
    x = tokens[0]
    odd = (lax.axis_index("fsdp") % 2).astype(F32)
    six = jnp.stack([norm1_gain, norm1_bias, proj_bias, norm2_gain, norm2_bias, fc2_bias]).astype(F32)
    vec = jnp.concatenate([
        jnp.concatenate([six * (1.0 - odd), six * odd], axis=1), fc1_bias.astype(F32).reshape(2, 128),
        jnp.broadcast_to(adapter_ids[0].astype(F32)[:, None], (1, 128)), jnp.zeros((7, 128), F32)], axis=0)
    (wq, wp, vecf, qkv, n1, c1, prob, oh, att, c2, gm, gf, out) = run_forward(
        segments, adapter_ids, x, vec, qkv_down, proj_down, proj_up, w_qkv, w_proj, w_fc1, w_fc2, qkv_up,
        grad_out[0], fc1_up, fc1_down, fc2_up, fc2_down)
    gall, gn = run_backward(segments, adapter_ids, gm, att, c2, oh, proj_down, proj_up, qkv_down, gf, wp, wq, qkv, n1, c1, prob, qkv_up)
    gt, gqd, gqu, gpd, gpu, gf1d, gf1u, gf2d, gf2u = run_expand(vecf, gall, gn, x, gm)
    return out[None], gt[None], gqd, gqu, gpd, gpu, gf1d, gf1u, gf2d, gf2u


def solution(mesh):
    sizes = dict(mesh.shape)
    small = sizes == {"seq": 2, "fsdp": 16}

    def per_device_any(*args):
        tokens, adapter_ids = args[0], args[4]
        one_image = tokens.shape[1:] == (512, 1024) and adapter_ids.shape[1] == 1
        return (per_device_fast if small and one_image else per_device)(*args)

    return jax.shard_map(
        per_device_any,
        mesh=mesh,
        in_specs=(
            P("fsdp", "seq", None),
            P("fsdp", "seq", None),
            P("fsdp", None),
            P("fsdp", None),
            P("fsdp", None),
            P("fsdp"),
            P("fsdp"),
            P("fsdp", None),
            P("fsdp", None),
            P("fsdp"),
            P("fsdp"),
            P("fsdp"),
            P("fsdp", None),
            P("fsdp"),
            P("fsdp", None),
            P("fsdp"),
            P(),
            P(),
            P(),
            P(),
            P(),
            P(),
            P(),
            P(),
        ),
        out_specs=(
            P("fsdp", "seq", None),
            P("fsdp", "seq", None),
            P(),
            P(),
            P(),
            P(),
            P(),
            P(),
            P(),
            P(),
        ),
        check_vma=False,
    )
```

profile of v0, /device:TPU:11, one launch (start us, length us, event | category | flops | bytes accessed | tf_op | source)
XLA Modules:
  0.0 289.8 jit_solution(10014008454969238729)
XLA Ops:
  1.3 0.1 pad.3.clone
  1.4 0.1 pad.4.clone
  1.5 0.7 bitcast_convert_fusion
  2.1 0.8 stack.27
  2.9 0.7 maximum_maximum_fusion.vec_ref
  3.6 155.7 %forward.1 = (bf16[1024,1536]{1,0:T(8,128)(2,1)}, bf16[1024,1024]{1,0:T(8,128)(2,1)}, f32[256,128]{1,0:T(8,128)}, bf16[640,1536]{1,0:T(8,128)(2,1)}, bf16[640,10...) custom-call(s32[1,1024]{1,0:T(1,128)} %seg_ref.3, ...), custom_call_target="tpu_custom_call" | custom-call | tf_op jit(solution)/shard_map/forward/pallas_call | solution.py:946
  159.3 119.8 %backward.1 = (bf16[256,16384]{1,0:T(8,128)(2,1)}, f32[512,1024]{1,0:T(8,128)}) custom-call(s32[1,1024]{1,0:T(1,128)} %seg_ref.3, s32[1,1]{1,0:T(1,128)S(6)} %copy.34.id_ref, f32[512,1024]{1,0:T(8,128)} %get-tuple-element.36.gm_ref.gm, bf16[512,1024]{1,0:T(8,128)(2,1)} %get-tuple-element.37.att_ref, bf16[512,128]{1,0:T(8,128)(2,1)} %get-tuple-element.38.c2_ref, ...), custom_call_target="tpu_custom_call" | custom-call | tf_op jit(solution)/shard_map/backward/pallas_call | solution.py:1129
  279.1 0.0 copy-start
  279.1 9.7 %expand.1 = (f32[512,1024]{1,0:T(8,128)}, f32[1024,128]{1,0:T(8,128)}, f32[128,3072]{1,0:T(8,128)}, f32[1024,128]{1,0:T(8,128)}, f32[128,1024]{1,0:T(8,128)}, /*...) custom-call(f32[256,128]{1,0:T(8,128)} %get-tuple-element.35.vec_ref, ...), custom_call_target="tpu_custom_call" | custom-call | tf_op jit(solution)/shard_map/expand/pallas_call | solution.py:1168
  288.8 0.0 copy-done
  288.8 1.0 copy.35
  (2 shorter events, 0.0 us)
Async XLA Ops:
  279.1 9.7 %copy-start = (bf16[512,1024]{1,0:T(8,128)(2,1)S(1)}, bf16[512,1024]{1,0:T(8,128)(2,1)}, u32[]{:S(2)}) copy-start(bf16[512,1024]{1,0:T(8,128)(2,1)} %get-tuple-element.34) | copy-start | bytes 3145732
where the time goes:
time: 293 us; the launch traced here: 290 us
  Pallas kernels  285 us (97%)
    pallas_call x1, Pallas kernels, run_forward(): pl.pallas_call(forward_kernel, out_shape=out_shape, in_specs=[vmem_spec()...  156 us
    pallas_call x1, Pallas kernels, run_backward(): pl.pallas_call(backward_kernel, out_shape=out_shape, in_specs=[vmem_spec(...  120 us
    pallas_call x1, Pallas kernels, run_expand(): pl.pallas_call(expand_kernel, grid=(n,), out_shape=(sds((rows, width), F3...  9.71 us

commit v1 on v0

--- a/solution.py
+++ b/solution.py
@@ -384,16 +384,24 @@
     def z_peer(self, d):
         return {"fsdp": self.block((self.z + d) % 4, self.x, self.c)}
 
-    def barrier(self):
+    def meet(self, peers):
         sem = pltpu.get_barrier_semaphore()
-        peers = [self.partner, self.x_peer, self.c_peer] + [self.z_peer(d) for d in (1, 2, 3)]
         for peer in peers:
             pl.semaphore_signal(sem, inc=1, device_id=peer, device_id_type=MESH)
         pl.semaphore_wait(sem, len(peers))
 
+    def plane_peer(self, d):
+        return {"fsdp": (self.f + d) % 16}
+
+    def plane_barrier(self):
+        self.meet([self.partner] + [self.plane_peer(d) for d in range(1, 16)])
+
+    def barrier(self):
+        self.meet([self.partner, self.x_peer, self.c_peer] + [self.z_peer(d) for d in (1, 2, 3)])
+
 
 class Block:
-    def __init__(self, src, piece, send_sem, recv_sem, own_sem, plane=None):
+    def __init__(self, src, piece, send_sem, recv_sem, own_sem, plane=2):
         self.src, self.piece, self.plane = src, piece, plane
         self.send_sem, self.recv_sem, self.own_sem = send_sem, recv_sem, own_sem
 
@@ -413,10 +421,22 @@
         return piece
 
     def here(self, it, body):
-        if it.plane is None:
+        if isinstance(it.plane, int) and it.plane == 2:
             body()
         else:
-            pl.when(self.net.s == it.plane)(body)
+            pl.when((self.net.s == it.plane) | (it.plane == 2))(body)
+
+    def hand_on(self, it, copies):
+        if isinstance(it.plane, int):
+            if it.plane != 2:
+                for copy in copies:
+                    copy.start()
+            return
+
+        @pl.when(it.plane != 2)
+        def _():
+            for copy in copies:
+                copy.start()
 
     def own(self, it):
         return pltpu.make_async_copy(it.src, it.piece(self.net.f), it.own_sem)
@@ -437,13 +457,14 @@
         net = self.net
 
         def body():
+            pieces = []
             for n, d in enumerate((1, 3, 2)):
                 block = net.block((net.z + d) % 4, net.x, net.c)
                 piece = self.arrive(it, block)
                 self.copy(it, piece, block, 5 + 2 * n, net.x_peer).start()
-                if it.plane is not None:
-                    self.copy(it, piece, block, 15 + n, net.partner).start()
                 self.copy(it, piece, block, 6 + 2 * n, net.c_peer).start()
+                pieces.append((piece, block))
+            self.hand_on(it, [self.copy(it, piece, block, 15 + n, net.partner) for n, (piece, block) in enumerate(pieces)])
 
         self.here(it, body)
 
@@ -451,21 +472,22 @@
         net = self.net
 
         def body():
+            pieces = []
             for n, d in enumerate((0, 1, 3, 2)):
                 block = net.block((net.z + d) % 4, 1 - net.x, net.c)
                 piece = self.arrive(it, block)
-                if it.plane is not None:
-                    self.copy(it, piece, block, 18 + n, net.partner).start()
                 self.copy(it, piece, block, 11 + n, net.c_peer).start()
+                pieces.append((piece, block))
+            self.hand_on(it, [self.copy(it, piece, block, 18 + n, net.partner) for n, (piece, block) in enumerate(pieces)])
 
         self.here(it, body)
 
     def from_seq(self, it):
         net = self.net
-        if it.plane is None:
+        if isinstance(it.plane, int) and it.plane == 2:
             return
 
-        @pl.when(net.s != it.plane)
+        @pl.when((net.s != it.plane) & (it.plane != 2))
         def _():
             for n, (d, x) in enumerate(((1, net.x), (3, net.x), (2, net.x), (0, 1 - net.x), (1, 1 - net.x),
                                         (3, 1 - net.x), (2, 1 - net.x))):
@@ -490,15 +512,19 @@
             def _(k):
                 self.copy(it, it.src, net.f, k, net.c_peer).wait_send()
 
-        if it.plane is None:
+        if isinstance(it.plane, int) and it.plane == 2:
             sent(0, 15)
             return
+
+        @pl.when(it.plane == 2)
+        def _():
+            sent(0, 15)
 
         @pl.when(net.s == it.plane)
         def _():
             sent(0, 22)
 
-        @pl.when(net.s != it.plane)
+        @pl.when((net.s != it.plane) & (it.plane != 2))
         def _():
             sent(4, 12)
 
@@ -568,7 +594,8 @@
 
 N_FC1 = 8
 N_FC2 = 4
-N_ITEMS = 3 + N_FC2 + N_FC1
+FIRST = 6
+N_ITEMS = FIRST + N_FC2 + N_FC1
 
 
 def forward_kernel(seg_ref, id_ref, x_ref, vec_ref, qd_ref, pd_ref, pu_ref, wq_hbm, wp_hbm, w1_hbm, w2_hbm,
@@ -612,38 +639,57 @@
     for copy in pre:
         copy.wait()
 
-    def block(n, src, piece, plane=None):
+    def block(n, src, piece, plane=2):
         return Block(src, piece, lambda k: g_send.at[n, k], lambda b: g_recv.at[n, b], g_own.at[n], plane)
 
+    def wq_part(part):
+        cols = pl.ds(part * half, half)
+        return block(1 + part, wq_own.at[:, cols], lambda b: wq.at[pl.ds(b * rb, rb), cols])
+
+    def wp_part(part):
+        cols = pl.ds(part * half, half)
+        return block(4 + part, wp_hbm.at[:, cols], lambda b: wp.at[pl.ds(b * rb, rb), cols], part)
+
     sub = fr2 // N_FC2
-    vec_it = block(0, vec_ref, lambda b: vecf.at[pl.ds(b * 16, 16), :])
-    wq_it = block(1, wq_own, lambda b: wq.at[pl.ds(b * rb, rb), :])
-    wp_it = block(2, wp_hbm, lambda b: wp.at[pl.ds(b * rb, rb), :])
-    fc2_it = [block(3 + j, w2_hbm.at[pl.ds(j * sub, sub), :], lambda b, j=j: w2.at[pl.ds(b * fr2 + j * sub, sub), :],
-                    (0, 1, None, None)[j]) for j in range(N_FC2)]
+
+    def times(j, size):
+        return j * size if isinstance(j, int) else pl.multiple_of(j * size, size)
+
+    def item(n):
+        if isinstance(n, int) and n < FIRST:
+            if n == 0:
+                return block(0, vec_ref, lambda b: vecf.at[pl.ds(b * 16, 16), :])
+            return wq_part(n - 1) if n < 4 else wp_part(n - 4)
+        if isinstance(n, int):
+            return fc2_it(n - FIRST) if n < FIRST + N_FC2 else fc1_it(n - FIRST - N_FC2)
+        return fc1_it(n - FIRST - N_FC2)
+
+    def fc2_it(j):
+        at = pl.ds(times(j, sub), sub)
+        return block(FIRST + j, w2_hbm.at[at, :], lambda b: w2.at[pl.ds(b * fr2 + times(j, sub), sub), :],
+                     (0, 1, 2, 2)[j])
 
     def fc1_it(j):
-        cols = pl.ds(j * FFB if isinstance(j, int) else pl.multiple_of(j * FFB, FFB), FFB)
-        return block(3 + N_FC2 + j, w1_hbm.at[:, cols], lambda b: w1.at[pl.ds(b * fr1, fr1), cols], j % 2)
+        cols = pl.ds(times(j, FFB), FFB)
+        return block(FIRST + N_FC2 + j, w1_hbm.at[:, cols], lambda b: w1.at[pl.ds(b * fr1, fr1), cols],
+                     ((2, 2, 0, 1)[j % 4] if isinstance(j, int) else jnp.where(j % 4 < 2, 2, j % 4 - 2)))
 
     gather = Gather(net)
-    gather.start(vec_it)
-    gather.start(wq_it)
+    stages = {"S": gather.start, "A": gather.from_z, "B": gather.from_x, "Y": gather.from_seq, "C": gather.from_core}
+
+    def go(*steps):
+        for step in steps:
+            stages[step[0]](item(int(step[1:])))
+
+    go("S0", "S1", "S2")
     image = Image(seg_ref, id_ref)
     zeros = jnp.zeros((PAD, 128), BF16)
     opad[0:PAD, :] = zeros
     opad[PAD + WINDOW:2 * PAD + WINDOW, :] = zeros
-    gather.from_z(vec_it)
-    gather.from_z(wq_it)
-    gather.start(wp_it)
-    gather.from_x(vec_it)
-    gather.from_x(wq_it)
-    gather.start(fc2_it[0])
-    gather.start(fc2_it[1])
+    go("A0", "A1", "S3", "A2", "S4", "S5", "B0", "B1", "A3", "S6", "S7", "B2", "A4", "A5", "S8")
     for copy in late:
         copy.wait()
-    gather.from_core(vec_it)
-    gather.from_core(wq_it)
+    go("B3", "C0", "C1", "C2", "C3")
 
     gain1 = full_vector(vecf, 0)
     shift1 = full_vector(vecf, 1)
@@ -660,23 +706,18 @@
             cols = pl.ds(part * half, half)
             qkv[at, cols] = (mm(normed, wq[:, cols]) + mm(inner, qu[:, cols])).astype(BF16)
 
-    @pl.loop(0, 2)
-    def _(i):
-        project(x_ref, pl.multiple_of(i * chunk, chunk), pl.multiple_of(s * rows + i * chunk, chunk))
-
-    gather.from_z(wp_it)
-    gather.start(fc2_it[2])
-
-    @pl.loop(0, 2)
-    def _(i):
-        pltpu.make_async_remote_copy(
-            src_ref=x_ref.at[pl.ds(0, chunk), :], dst_ref=xp.at[pl.ds(0, chunk), :], send_sem=xs_sem.at[i],
-            recv_sem=xr_sem.at[i], device_id=net.partner, device_id_type=MESH).wait_recv()
-        project(xp, pl.multiple_of(i * chunk, chunk), pl.multiple_of(other * rows + i * chunk, chunk))
-
-    gather.from_x(wp_it)
-    gather.from_z(fc2_it[0])
-    gather.from_z(fc2_it[1])
+    def own_rows_in(i):
+        project(x_ref, i * chunk, pl.multiple_of(s * rows + i * chunk, chunk))
+
+    def partner_rows_in(i):
+        x_copy(i).wait_recv()
+        project(xp, i * chunk, pl.multiple_of(other * rows + i * chunk, chunk))
+
+    own_rows_in(0)
+    own_rows_in(1)
+    partner_rows_in(0)
+    partner_rows_in(1)
+    go("B4", "B5", "A6", "A7", "S9")
     outs = []
 
     def put(src, dst):
@@ -715,6 +756,11 @@
     def _(pair):
         def cols(part):
             return pl.ds(pl.multiple_of(part * half + pair * 128, 128), 128)
+
+        for n, steps in enumerate(((), ("Y4", "Y5"), ("B6", "B7", "A8", "S10", "S11"), ("C4", "C5"))):
+            @pl.when(pair == n)
+            def _(steps=steps):
+                go(*steps)
 
         k2 = qkvw[:, cols(1)]
         v2 = qkvw[:, cols(2)]
@@ -751,29 +797,7 @@
         att_copy(pair).start()
         att[:, pl.ds(pl.multiple_of(s * half + pair * 128, 128), 128)] = own_rows(s)
 
-        @pl.when(pair == 0)
-        def _():
-            gather.from_core(wp_it)
-            gather.from_x(fc2_it[0])
-            gather.from_x(fc2_it[1])
-
-        @pl.when(pair == 1)
-        def _():
-            gather.start(fc2_it[3])
-            gather.from_z(fc2_it[2])
-
-        @pl.when(pair == 2)
-        def _():
-            gather.from_seq(fc2_it[0])
-            gather.from_seq(fc2_it[1])
-            gather.start(fc1_it(0))
-            gather.start(fc1_it(1))
-
-        @pl.when(pair == 3)
-        def _():
-            gather.from_x(fc2_it[2])
-            gather.from_z(fc2_it[3])
-
+    go("B8", "A9", "S12", "S13", "Y6", "Y7")
     put(wp, wpf)
     put(oh, oh_out)
 
@@ -782,6 +806,7 @@
         att_copy(pair).wait_recv()
 
     put(att, att_out)
+    go("A10", "S14")
     bias_p = full_vector(vecf, 2)
     gain2 = full_vector(vecf, 3)
     shift2 = full_vector(vecf, 4)
@@ -811,37 +836,10 @@
     c3t[...] = c3[...].T
     e4t[...] = e4[...].T
     put(c2, c2_out)
-    gather.start(fc1_it(2))
-    gather.from_z(fc1_it(0))
-    gather.from_z(fc1_it(1))
-    gather.from_x(fc2_it[3])
-    gather.start(fc1_it(3))
-    gather.from_x(fc1_it(0))
-    gather.from_x(fc1_it(1))
-    gather.from_z(fc1_it(2))
-    gather.start(fc1_it(4))
-    for j in range(N_FC2):
-        gather.from_core(fc2_it[j])
-    gather.from_seq(fc1_it(0))
+    go("B9", "A11", "S15", "C6", "C7", "C8", "C9", "B10", "A12", "A13", "S16", "S17", "B11")
 
     @pl.loop(0, N_FC1)
     def _(j):
-        @pl.when(j + 5 < N_FC1)
-        def _():
-            gather.start(fc1_it(j + 5))
-
-        @pl.when(j + 3 < N_FC1)
-        def _():
-            gather.from_z(fc1_it(j + 3))
-
-        @pl.when(j + 2 < N_FC1)
-        def _():
-            gather.from_x(fc1_it(j + 2))
-
-        @pl.when(j + 1 < N_FC1)
-        def _():
-            gather.from_seq(fc1_it(j + 1))
-
         gather.from_core(fc1_it(j))
         bias = jnp.concatenate([vecf[pl.ds(2 * j * 16 + 6, 1), :], vecf[pl.ds(2 * j * 16 + 7, 1), :],
                                 vecf[pl.ds((2 * j + 1) * 16 + 6, 1), :], vecf[pl.ds((2 * j + 1) * 16 + 7, 1), :]], axis=1)
@@ -849,6 +847,14 @@
 
         @pl.loop(0, 2)
         def _(i):
+            @pl.when((i == 1) & (j + 4 < N_FC1))
+            def _():
+                gather.from_z(fc1_it(j + 4))
+
+            @pl.when((i == 1) & (j + 2 < N_FC1))
+            def _():
+                gather.from_x(fc1_it(j + 2))
+
             at = pl.ds(pl.multiple_of(i * chunk, chunk), chunk)
             hidden = mm(n2[at, :], w1[:, col]) + mm(c3[at, :], u1[:, col]) + bias
             cdf = 0.5 * (1.0 + lax.erf(hidden * (0.5 ** 0.5)))
@@ -863,6 +869,10 @@
             gacc[at, :] += mm_nt(grad_hidden, w1[:, col])
             e3[at, :] += mm_nt(grad_hidden, u1[:, col])
 
+        @pl.when(j + 1 < N_FC1)
+        def _():
+            gather.from_seq(fc1_it(j + 1))
+
         gr[:, col] = compact_rows(mm(c3t[...], gh_s[...]))
         gr[:, pl.ds(pl.multiple_of(ff + j * FFB, FFB), FFB)] = compact_rows(mm(e4t[...], act_s[...]))
 
@@ -897,8 +907,8 @@
     def _(pair):
         att_copy(pair).wait_send()
 
-    for it in [vec_it, wq_it, wp_it] + fc2_it:
-        gather.finish(it)
+    for n in range(FIRST + N_FC2):
+        gather.finish(item(n))
 
     @pl.loop(0, N_FC1)
     def _(j):
@@ -950,12 +960,23 @@
         name="forward")(seg, ident, x, vec, qd, pd, pu, wq, wp, w1, w2, qu, g, u1, d1, u2, d2)
 
 
-def backward_kernel(seg_ref, id_ref, gm_ref, att_ref, c2_ref, oh_ref, pd_ref, pu_ref, qd_ref, gf_ref, wp_ref,
+FIRST_PARTS = 3
+
+
+def adapter_rows(vec_ref):
+    ids = jnp.concatenate([jnp.broadcast_to(vec_ref[16 * p + 8:16 * p + 9, :], (16, 128)) for p in range(16)], axis=0)
+    r = lax.broadcasted_iota(jnp.int32, (256, 128), 0) % 16
+    col = lax.broadcasted_iota(jnp.int32, (256, 128), 1)
+    group = (col // 16).astype(F32)
+    return ((ids == group) & (r == col % 16)).astype(F32).T.astype(BF16)
+
+
+def backward_kernel(seg_ref, id_ref, vec_ref, gm_ref, att_ref, c2_ref, oh_ref, pd_ref, pu_ref, qd_ref, gf_ref, wp_ref,
                     wq_hbm, qkv_hbm, n1_hbm, c1_hbm, prob_hbm, qu_hbm,
                     gall, gn_out,
-                    wq, qkv, n1, c1, prob, qu, g1, e2, gsend, do_s, first_own, first_send, first_in, gq, qsend, qdown, qdown_in, qown,
-                    gpad, psend, prcv, gn,
-                    loc_sem, ds_sem, dr_sem, fs_sem, fr_sem, qs_sem, qr_sem, ps_sem, pr_sem, out_sem, g_send, g_recv, g_own):
+                    wq, qkv, n1, c1, prob, qu, g1, e2, gsend, do_s, first_own, first_in, last_own, last_in, first_sum, last_sum,
+                    parts1, parts2, dense1, dense2, gq, gpad, psend, prcv, gn,
+                    loc_sem, ds_sem, dr_sem, fs_sem, fr_sem, ps_sem, pr_sem, out_sem, t_send, t_recv, g_send, g_recv, g_own):
     net = Net()
     s, other = net.s, 1 - net.s
     image = Image(seg_ref, id_ref)
@@ -963,6 +984,8 @@
     half = wq.shape[1] // 3
     chunk = rows // 2
     ffn_cols = gf_ref.shape[1]
+    n_first = first_own.shape[1]
+    own1, own2 = n_first // 16, 4 * width // 16
 
     loads = [pltpu.make_async_copy(src, dst, loc_sem.at[i]) for i, (src, dst) in enumerate(
         [(qkv_hbm, qkv), (prob_hbm, prob), (wq_hbm, wq), (n1_hbm, n1), (c1_hbm, c1)])]
@@ -971,7 +994,11 @@
         loads.append(pltpu.make_async_copy(qu_hbm.at[:, cols], qu.at[:, pl.ds(part * half, half)], loc_sem.at[5 + part]))
     for copy in loads:
         copy.start()
-    net.barrier()
+    net.plane_barrier()
+
+    def to_partner(src, dst, send, recv):
+        return pltpu.make_async_remote_copy(src_ref=src, dst_ref=dst, send_sem=send, recv_sem=recv,
+                                            device_id=net.partner, device_id_type=MESH)
 
     @pl.loop(0, 2)
     def _(i):
@@ -988,46 +1015,97 @@
     dsend = []
     for i in range(2):
         gsend[i] = grad_att(i, other)
-        copy = pltpu.make_async_remote_copy(
-            src_ref=gsend.at[i], dst_ref=do_s.at[pl.ds(pl.multiple_of(s * rows + i * chunk, chunk), chunk), :],
-            send_sem=ds_sem.at[i], recv_sem=dr_sem.at[i], device_id=net.partner, device_id_type=MESH)
+        copy = to_partner(gsend.at[i], do_s.at[pl.ds(pl.multiple_of(s * rows + i * chunk, chunk), chunk), :],
+                          ds_sem.at[i], dr_sem.at[i])
         copy.start()
         dsend.append(copy)
     first_own[:, 0:ffn_cols] = gf_ref[...]
     first_own[:, ffn_cols:ffn_cols + width] = compact_rows(mm_tn(c2_ref[...], g1[...]))
     first_own[:, ffn_cols + width:ffn_cols + 2 * width] = compact_rows(mm_tn(e2[...].astype(BF16), att_ref[...]))
-    fsend = pltpu.make_async_remote_copy(
-        src_ref=first_own, dst_ref=first_in, send_sem=fs_sem.at[0], recv_sem=fr_sem.at[0],
-        device_id=net.partner, device_id_type=MESH)
+    fsend = to_partner(first_own, first_in, fs_sem.at[0], fr_sem.at[0])
     fsend.start()
     for i in range(2):
         do_s[pl.ds(pl.multiple_of(s * rows + i * chunk, chunk), chunk), :] = grad_att(i, s)
-    n_first = first_own.shape[1]
-    items = [Block(src, lambda b, cols=cols: gall.at[pl.ds(b * 16, 16), cols], lambda k, n=n: g_send.at[n, k],
-                   lambda b, n=n: g_recv.at[n, b], g_own.at[n])
-             for n, (src, cols) in enumerate(((first_send, pl.ds(0, n_first)), (qown, pl.ds(n_first, 4 * width))))]
-    gather = Gather(net)
     zeros = jnp.zeros((PAD, width), F32)
     gpad[0:PAD, :] = zeros
     gpad[PAD + WINDOW:2 * PAD + WINDOW, :] = zeros
+    last_own[...] = jnp.zeros_like(last_own)
+    pick = adapter_rows(vec_ref)
+
+    def turn(n, src, dst, cols, d):
+        peer = (net.f + d) % 16
+        return pltpu.make_async_remote_copy(
+            src_ref=src.at[:, pl.ds(pl.multiple_of(peer * cols, 128), cols)],
+            dst_ref=dst.at[pl.ds(pl.multiple_of(net.f * 16, 16), 16), :], send_sem=t_send.at[n, d],
+            recv_sem=t_recv.at[n, net.f], device_id={"fsdp": peer}, device_id_type=MESH)
+
+    def turn_start(n, src, dst, cols):
+        @pl.loop(1, 16)
+        def _(d):
+            turn(n, src, dst, cols, d).start()
+
+        dst[pl.ds(pl.multiple_of(net.f * 16, 16), 16), :] = src[:, pl.ds(pl.multiple_of(net.f * cols, 128), cols)]
+
+    def turn_wait(n, src, dst, cols):
+        @pl.loop(1, 16)
+        def _(d):
+            peer = (net.f + d) % 16
+            pltpu.make_async_remote_copy(
+                src_ref=src.at[:, pl.ds(0, cols)], dst_ref=dst.at[pl.ds(pl.multiple_of(peer * 16, 16), 16), :],
+                send_sem=t_send.at[n, d], recv_sem=t_recv.at[n, peer], device_id={"fsdp": peer},
+                device_id_type=MESH).wait_recv()
+
+    def turn_finish(n, src, dst, cols):
+        @pl.loop(1, 16)
+        def _(d):
+            turn(n, src, dst, cols, d).wait_send()
+
+    def block(n, src, first, step, cols):
+        return Block(src, lambda b: gall.at[:, pl.ds(pl.multiple_of(first + b * step, 128), cols)],
+                     lambda k: g_send.at[n, k], lambda b: g_recv.at[n, b], g_own.at[n])
+
+    share = own1 // FIRST_PARTS
+    items = [block(n, dense1.at[:, pl.ds(n * share, share)], n * share, own1, share) for n in range(FIRST_PARTS)]
+    items.append(block(FIRST_PARTS, dense2, n_first, own2, own2))
+    gather = Gather(net)
+    stages = {"S": gather.start, "A": gather.from_z, "B": gather.from_x, "C": gather.from_core}
+
+    def go(*steps):
+        for step in steps:
+            stages[step[0]](items[int(step[1:])])
+
     for copy in loads:
         copy.wait()
     for copy in dsend:
         copy.wait_recv()
-    fsend.wait_recv()
-    first_send[...] = (first_own[...].astype(F32) + first_in[...].astype(F32)).astype(BF16)
-    gather.start(items[0])
 
     halves = lane_halves()
     scale = HEAD_DIM ** (-0.5)
     keep = image.inside((WINDOW, 1), 0).astype(BF16)
-    for pair in range(half // 128):
-        cols = slice(pair * 128, (pair + 1) * 128)
-        k2 = qkv[:, half + pair * 128:half + (pair + 1) * 128]
-        v2 = qkv[:, 2 * half + pair * 128:2 * half + (pair + 1) * 128]
-        q2 = qkv[:, cols] * jnp.asarray(scale, BF16)
-        do2 = image.choose(lambda at: do_s[at:at + WINDOW, cols]) * keep
-        inner = do2.astype(F32) * oh_ref[:, cols].astype(F32)
+
+    @pl.loop(0, half // 128)
+    def _(pair):
+        @pl.when(pair == 1)
+        def _():
+            fsend.wait_recv()
+            first_sum[...] = (first_own[...].astype(F32) + first_in[...].astype(F32)).astype(BF16)
+            turn_start(0, first_sum, parts1, own1)
+
+        @pl.when(pair == 3)
+        def _():
+            turn_wait(0, first_sum, parts1, own1)
+            for n in range(FIRST_PARTS):
+                dense1[:, n * share:(n + 1) * share] = mm(pick, parts1[:, n * share:(n + 1) * share]).astype(BF16)
+            go("S0", "S1", "S2")
+
+        def cols(part):
+            return pl.ds(pl.multiple_of(part * half + pair * 128, 128), 128)
+
+        k2 = qkv[:, cols(1)]
+        v2 = qkv[:, cols(2)]
+        q2 = qkv[:, cols(0)] * jnp.asarray(scale, BF16)
+        do2 = image.choose(lambda at: do_s[at:at + WINDOW, cols(0)]) * keep
+        inner = do2.astype(F32) * oh_ref[:, cols(0)].astype(F32)
         gv = gk = gqq = None
         for hd in range(2):
             hm = halves[hd].astype(BF16)
@@ -1041,31 +1119,17 @@
             gv = dv if gv is None else gv + dv
             gk = dk if gk is None else gk + dk
             gqq = dq if gqq is None else gqq + dq
-        gq[:, cols] = (gqq * scale).astype(BF16)
-        gq[:, half + pair * 128:half + (pair + 1) * 128] = gk.astype(BF16)
-        gq[:, 2 * half + pair * 128:2 * half + (pair + 1) * 128] = gv.astype(BF16)
-        if pair == 1:
-            gather.from_z(items[0])
-        if pair == 2:
-            gather.from_x(items[0])
+        gq[:, cols(0)] = (gqq * scale).astype(BF16)
+        gq[:, cols(1)] = gk.astype(BF16)
+        gq[:, cols(2)] = gv.astype(BF16)
 
     up = compact_rows(mm_tn(c1[...], gq[...]))
     e1 = (mm_nt(gq[...], qu[...]) * image.select_window(0, WINDOW)).astype(BF16)
-    down = mm_tn(e1, n1[...])
-    qdown[...] = compact_rows(down)
-    qsends = []
     for part in range(3):
-        cols = pl.ds(pl.multiple_of(part * width + s * half, 128), half)
-        qsend[:, pl.ds(part * half, half)] = up[:, part * half:(part + 1) * half]
-        qown[:, cols] = up[:, part * half:(part + 1) * half]
-        qsends.append(pltpu.make_async_remote_copy(
-            src_ref=qsend.at[:, pl.ds(part * half, half)], dst_ref=qown.at[:, cols], send_sem=qs_sem.at[part],
-            recv_sem=qr_sem.at[part], device_id=net.partner, device_id_type=MESH))
-    qsends.append(pltpu.make_async_remote_copy(
-        src_ref=qdown, dst_ref=qdown_in, send_sem=qs_sem.at[3],
-        recv_sem=qr_sem.at[3], device_id=net.partner, device_id_type=MESH))
-    for copy in qsends:
-        copy.start()
+        last_own[:, pl.ds(pl.multiple_of(part * width + s * half, 128), half)] = up[:, part * half:(part + 1) * half]
+    last_own[:, 3 * width:4 * width] = compact_rows(mm_tn(e1, n1[...]))
+    lsend = to_partner(last_own, last_in, fs_sem.at[1], fr_sem.at[1])
+    lsend.start()
 
     @pl.loop(0, 2)
     def _(i):
@@ -1073,78 +1137,76 @@
         e1_rows = (mm_nt(gq[at, :], qu[...]) * image.select_window(i * QROWS, QROWS)).astype(BF16)
         gpad[pl.ds(pl.multiple_of(PAD + i * QROWS, STEP), QROWS), :] = mm_nt(gq[at, :], wq[...]) + mm_nt(e1_rows, qd_ref[...])
 
+    def rows_of(who, i):
+        return image.choose(lambda at: gpad[pl.ds(pl.multiple_of(who * rows + PAD + i * chunk - at, STEP), chunk), :])
+
     psends = []
     for i in range(2):
-        psend[i] = image.choose(lambda at: gpad[
-            pl.ds(pl.multiple_of(other * rows + PAD + i * chunk - at, STEP), chunk), :]).astype(BF16)
-        copy = pltpu.make_async_remote_copy(
-            src_ref=psend.at[i], dst_ref=prcv.at[i], send_sem=ps_sem.at[i], recv_sem=pr_sem.at[i],
-            device_id=net.partner, device_id_type=MESH)
+        psend[i] = rows_of(other, i).astype(BF16)
+        copy = to_partner(psend.at[i], prcv.at[i], ps_sem.at[i], pr_sem.at[i])
         copy.start()
         psends.append(copy)
-    for copy in qsends:
-        copy.wait_recv()
-    qown[:, 3 * width:4 * width] = (qdown[...].astype(F32) + qdown_in[...].astype(F32)).astype(BF16)
-    gather.start(items[1])
-    gather.from_core(items[0])
-    gather.from_z(items[1])
-    gather.from_x(items[1])
-    gather.from_core(items[1])
+    go("A0")
+    lsend.wait_recv()
+    last_sum[...] = (last_own[...].astype(F32) + last_in[...].astype(F32)).astype(BF16)
+    turn_start(1, last_sum, parts2, own2)
+    go("A1", "B0", "A2", "B1")
+    turn_wait(1, last_sum, parts2, own2)
+    dense2[...] = mm(pick, parts2[...]).astype(BF16)
+    go("S3", "B2", "C0", "C1", "A3", "C2", "B3")
     outs = []
     for i in range(2):
         psends[i].wait_recv()
         rows_at = pl.ds(i * chunk, chunk)
-        gn[rows_at, :] = prcv[i].astype(F32) + image.choose(lambda at: gpad[
-            pl.ds(pl.multiple_of(s * rows + PAD + i * chunk - at, STEP), chunk), :])
+        gn[rows_at, :] = prcv[i].astype(F32) + rows_of(s, i)
         copy = pltpu.make_async_copy(gn.at[rows_at, :], gn_out.at[rows_at, :], out_sem.at[i])
         copy.start()
         outs.append(copy)
+    go("C3")
     for copy in outs:
         copy.wait()
-    for copy in dsend + [fsend] + qsends + psends:
+    for copy in dsend + [fsend, lsend] + psends:
         copy.wait_send()
+    turn_finish(0, first_sum, parts1, own1)
+    turn_finish(1, last_sum, parts2, own2)
     for it in items:
         gather.finish(it)
 
 
-def run_backward(seg, ident, gm, att, c2, oh, pd, pu, qd, gf, wp, wq, qkv, n1, c1, prob, qu):
+def run_backward(seg, ident, vec, gm, att, c2, oh, pd, pu, qd, gf, wp, wq, qkv, n1, c1, prob, qu):
     rows, width = gm.shape
     toks = 2 * rows
     half = width // 2
     dma = pltpu.SemaphoreType.DMA
     sds = jax.ShapeDtypeStruct
     n_first = gf.shape[1] + 2 * width
-    out_shape = (sds((256, n_first + 4 * width), BF16), sds((rows, width), F32))
+    out_shape = (sds((128, n_first + 4 * width), BF16), sds((rows, width), F32))
     chunk = rows // 2
+
+    def low(*shape):
+        return pltpu.VMEM(shape, BF16)
+
     scratch = [
-        pltpu.VMEM(wq.shape, BF16), pltpu.VMEM(qkv.shape, BF16), pltpu.VMEM(n1.shape, BF16), pltpu.VMEM(c1.shape, BF16),
-        pltpu.VMEM(prob.shape, BF16), pltpu.VMEM((128, 3 * half), BF16), pltpu.VMEM((rows, width), BF16),
-        pltpu.VMEM((rows, 128), F32), pltpu.VMEM((2, chunk, half), BF16), pltpu.VMEM((toks, half), BF16),
-        pltpu.VMEM((16, n_first), BF16), pltpu.VMEM((16, n_first), BF16), pltpu.VMEM((16, n_first), BF16),
-        pltpu.VMEM((WINDOW, 3 * half), BF16), pltpu.VMEM((16, 3 * half), BF16), pltpu.VMEM((16, width), BF16),
-        pltpu.VMEM((16, width), BF16), pltpu.VMEM((16, 4 * width), BF16), pltpu.VMEM((2 * PAD + WINDOW, width), F32), pltpu.VMEM((2, chunk, width), BF16),
-        pltpu.VMEM((2, chunk, width), BF16), pltpu.VMEM((rows, width), F32),
-        dma((8,)), dma((2,)), dma((2,)), dma((1,)), dma((1,)), dma((4,)), dma((4,)), dma((2,)), dma((2,)), dma((2,)),
-        dma((2, 15)), dma((2, 16)), dma((2,))]
+        low(*wq.shape), low(*qkv.shape), low(*n1.shape), low(*c1.shape), low(*prob.shape), low(128, 3 * half), low(rows, width),
+        pltpu.VMEM((rows, 128), F32), low(2, chunk, half), low(toks, half), low(16, n_first), low(16, n_first),
+        low(16, 4 * width), low(16, 4 * width), low(16, n_first), low(16, 4 * width), low(256, n_first // 16),
+        low(256, width // 4), low(128, n_first // 16), low(128, width // 4), low(WINDOW, 3 * half),
+        pltpu.VMEM((2 * PAD + WINDOW, width), F32), low(2, chunk, width), low(2, chunk, width), pltpu.VMEM((rows, width), F32),
+        dma((8,)), dma((2,)), dma((2,)), dma((2,)), dma((2,)), dma((2,)), dma((2,)), dma((2,)), dma((2, 16)), dma((2, 16)),
+        dma((FIRST_PARTS + 1, 22)), dma((FIRST_PARTS + 1, 16)), dma((FIRST_PARTS + 1,))]
     return pl.pallas_call(
-        backward_kernel, out_shape=out_shape,
-        in_specs=[vmem_spec()] * 11 + [any_spec()] * 6,
+        backward_kernel, out_shape=out_shape, in_specs=[vmem_spec()] * 12 + [any_spec()] * 6,
         out_specs=tuple(any_spec() for unused in out_shape), scratch_shapes=scratch,
         compiler_params=pltpu.CompilerParams(collective_id=2, has_side_effects=True, vmem_limit_bytes=VMEM_LIMIT),
-        name="backward")(seg, ident, gm, att, c2, oh, pd, pu, qd, gf, wp, wq, qkv, n1, c1, prob, qu)
+        name="backward")(seg, ident, vec, gm, att, c2, oh, pd, pu, qd, gf, wp, wq, qkv, n1, c1, prob, qu)
 
 
 def expand_kernel(vec_ref, f1u, f2d, f1d, f2u, pu, pdn, qu, qd, gn, x, gm,
                   gt_out, qd_out, qu_out, pd_out, pu_out, f1d_out, f1u_out, f2d_out, f2u_out):
-    ids = jnp.concatenate([jnp.broadcast_to(vec_ref[16 * p + 8:16 * p + 9, :], (16, 128)) for p in range(16)], axis=0)
-    r = lax.broadcasted_iota(jnp.int32, (256, 128), 0) % 16
-    col = lax.broadcasted_iota(jnp.int32, (256, 128), 1)
-    pick = ((ids.astype(jnp.int32) == col // 16) & (r == col % 16)).astype(F32)
-    pick_t = pick.T.astype(BF16)
     for src, dst in ((f1u, f1u_out), (f2u, f2u_out), (pu, pu_out), (qu, qu_out)):
-        dst[...] = mm(pick_t, src[...])
+        dst[...] = src[...].astype(F32)
     for src, dst in ((f1d, f1d_out), (f2d, f2d_out), (pdn, pd_out), (qd, qd_out)):
-        dst[...] = mm(pick_t, src[...]).T
+        dst[...] = src[...].astype(F32).T
     gain1 = full_vector(vec_ref, 0)
     gt_out[...] = gm[...] + norm_grad(x[...].astype(F32), gain1, gn[...])
 
@@ -1156,7 +1218,7 @@
     sds = jax.ShapeDtypeStruct
 
     def part(cols, offset):
-        return pl.BlockSpec((256, cols), lambda j: (0, offset // cols + j))
+        return pl.BlockSpec((128, cols), lambda j: (0, offset // cols + j))
 
     def by_row(shape):
         return pl.BlockSpec(shape, lambda j: (j, 0))
@@ -1191,7 +1253,7 @@
     (wq, wp, vecf, qkv, n1, c1, prob, oh, att, c2, gm, gf, out) = run_forward(
         segments, adapter_ids, x, vec, qkv_down, proj_down, proj_up, w_qkv, w_proj, w_fc1, w_fc2, qkv_up,
         grad_out[0], fc1_up, fc1_down, fc2_up, fc2_down)
-    gall, gn = run_backward(segments, adapter_ids, gm, att, c2, oh, proj_down, proj_up, qkv_down, gf, wp, wq, qkv, n1, c1, prob, qkv_up)
+    gall, gn = run_backward(segments, adapter_ids, vecf, gm, att, c2, oh, proj_down, proj_up, qkv_down, gf, wp, wq, qkv, n1, c1, prob, qkv_up)
     gt, gqd, gqu, gpd, gpu, gf1d, gf1u, gf2d, gf2u = run_expand(vecf, gall, gn, x, gm)
     return out[None], gt[None], gqd, gqu, gpd, gpu, gf1d, gf1u, gf2d, gf2u
 

time: 293 us -> 239 us (0.82)
  Pallas kernels: 285 us -> 234 us
    pallas_call x1, Pallas kernels: 120 us -> 77.7 us  [run_backward(): pl.pallas_call(backward_kernel, out_shape=out_shape, in_specs=[vmem_spec(...]
    pallas_call x1, Pallas kernels: 156 us -> 148 us  [run_forward(): pl.pallas_call(forward_kernel, out_shape=out_shape, in_specs=[vmem_spec()...]
where the time goes in v1:
time: 239 us
  Pallas kernels  234 us (98%)
    pallas_call x1, Pallas kernels, run_forward(): pl.pallas_call(forward_kernel, out_shape=out_shape, in_specs=[vmem_spec()...  148 us
    pallas_call x1, Pallas kernels, run_backward(): pl.pallas_call(backward_kernel, out_shape=out_shape, in_specs=[vmem_spec(...  77.7 us
    pallas_call x1, Pallas kernels, run_expand(): pl.pallas_call(expand_kernel, grid=(n,), out_shape=(sds((rows, width), F3...  8.58 us

profile of v1, /device:TPU:11, one launch (start us, length us, event | category | flops | bytes accessed | tf_op | source)
XLA Modules:
  0.0 238.6 jit_solution(9397734197686323110)
XLA Ops:
  1.3 0.1 pad.3.clone
  1.4 0.1 pad.4.clone
  1.5 0.7 bitcast_convert_fusion
  2.1 0.8 stack.27
  2.9 0.7 maximum_maximum_fusion.vec_ref
  3.6 147.8 %forward.1 = (bf16[1024,1536]{1,0:T(8,128)(2,1)}, bf16[1024,1024]{1,0:T(8,128)(2,1)}, f32[256,128]{1,0:T(8,128)}, bf16[640,1536]{1,0:T(8,128)(2,1)}, bf16[640,10...) custom-call(s32[1,1024]{1,0:T(1,128)} %seg_ref.3, ...), custom_call_target="tpu_custom_call" | custom-call | tf_op jit(solution)/shard_map/forward/pallas_call | solution.py:956
  151.3 77.7 %backward.1 = (bf16[128,16384]{1,0:T(8,128)(2,1)}, f32[512,1024]{1,0:T(8,128)}) custom-call(s32[1,1024]{1,0:T(1,128)} %seg_ref.3, s32[1,1]{1,0:T(1,128)S(6)} %copy.34.id_ref, f32[256,128]{1,0:T(8,128)} %get-tuple-element.35.vec_ref, f32[512,1024]{1,0:T(8,128)} %get-tuple-element.36.gm_ref.gm, bf16[512,1024]{1,0:T(8,128)(2,1)} %get-tuple-element.37.att_ref, ...), custom_call_target="tpu_custom_call" | custom-call | tf_op jit(solution)/shard_map/backward/pallas_call | solution.py:1197
  229.1 0.0 copy-start
  229.1 8.6 %expand.1 = (f32[512,1024]{1,0:T(8,128)}, f32[1024,128]{1,0:T(8,128)}, f32[128,3072]{1,0:T(8,128)}, f32[1024,128]{1,0:T(8,128)}, f32[128,1024]{1,0:T(8,128)}, /*...) custom-call(f32[256,128]{1,0:T(8,128)} %get-tuple-element.35.vec_ref, ...), custom_call_target="tpu_custom_call" | custom-call | tf_op jit(solution)/shard_map/expand/pallas_call | solution.py:1230
  237.7 0.0 copy-done
  237.7 1.0 copy.35
  (2 shorter events, 0.0 us)
Async XLA Ops:
  229.1 8.6 %copy-start = (bf16[512,1024]{1,0:T(8,128)(2,1)S(1)}, bf16[512,1024]{1,0:T(8,128)(2,1)}, u32[]{:S(2)}) copy-start(bf16[512,1024]{1,0:T(8,128)(2,1)} %get-tuple-element.34) | copy-start | bytes 3145732

commit v2 on v1

--- a/solution.py
+++ b/solution.py
@@ -339,7 +339,7 @@
 F32 = jnp.float32
 BF16 = jnp.bfloat16
 MESH = pl.DeviceIdType.MESH
-VMEM_LIMIT = 64 * 1000 * 1000
+VMEM_LIMIT = 67_000_000
 
 
 def mm(a, b):
@@ -401,24 +401,27 @@
 
 
 class Block:
-    def __init__(self, src, piece, send_sem, recv_sem, own_sem, plane=2):
-        self.src, self.piece, self.plane = src, piece, plane
-        self.send_sem, self.recv_sem, self.own_sem = send_sem, recv_sem, own_sem
+    def __init__(self, src, piece, some, sems, own_sem, plane=2):
+        self.src, self.piece, self.some, self.plane, self.own_sem = src, piece, some, plane, own_sem
+        self.sent, self.z, self.x, self.y1, self.y2, self.c = sems
+
+
+N_SEMS = 6
 
 
 class Gather:
     def __init__(self, net):
         self.net = net
 
-    def copy(self, it, src, block, k, peer):
+    def send(self, it, src, block, sem, peer):
+        pltpu.make_async_remote_copy(
+            src_ref=src, dst_ref=it.piece(block), send_sem=it.sent, recv_sem=sem, device_id=peer,
+            device_id_type=MESH).start()
+
+    def total(self, it, n, sem):
         return pltpu.make_async_remote_copy(
-            src_ref=src, dst_ref=it.piece(block), send_sem=it.send_sem(k), recv_sem=it.recv_sem(block),
-            device_id=peer, device_id_type=MESH)
-
-    def arrive(self, it, block):
-        piece = it.piece(block)
-        self.copy(it, piece, block, 0, self.net.c_peer).wait_recv()
-        return piece
+            src_ref=it.some(n), dst_ref=it.some(n), send_sem=it.sent, recv_sem=sem, device_id=self.net.c_peer,
+            device_id_type=MESH)
 
     def here(self, it, body):
         if isinstance(it.plane, int) and it.plane == 2:
@@ -426,45 +429,47 @@
         else:
             pl.when((self.net.s == it.plane) | (it.plane == 2))(body)
 
-    def hand_on(self, it, copies):
-        if isinstance(it.plane, int):
-            if it.plane != 2:
-                for copy in copies:
-                    copy.start()
-            return
-
-        @pl.when(it.plane != 2)
-        def _():
-            for copy in copies:
-                copy.start()
+    def hand_on(self, it, pieces, sem):
+        def body():
+            for piece, block in pieces:
+                self.send(it, piece, block, sem, self.net.partner)
+
+        if not isinstance(it.plane, int):
+            pl.when(it.plane != 2)(body)
+        elif it.plane != 2:
+            body()
 
     def own(self, it):
         return pltpu.make_async_copy(it.src, it.piece(self.net.f), it.own_sem)
 
+    def column(self, it, x, ds):
+        net = self.net
+        blocks = [net.block((net.z + d) % 4, x, net.c) for d in ds]
+        return [(it.piece(block), block) for block in blocks]
+
     def start(self, it):
         net = self.net
 
         def along():
             for d in (2, 1, 3):
-                self.copy(it, it.src, net.f, d - 1, net.z_peer(d)).start()
-            self.copy(it, it.src, net.f, 3, net.x_peer).start()
+                self.send(it, it.src, net.f, it.z, net.z_peer(d))
+            self.send(it, it.src, net.f, it.x, net.x_peer)
 
         self.here(it, along)
-        self.copy(it, it.src, net.f, 4, net.c_peer).start()
+        self.send(it, it.src, net.f, it.c, net.c_peer)
         self.own(it).start()
 
     def from_z(self, it):
         net = self.net
 
         def body():
-            pieces = []
-            for n, d in enumerate((1, 3, 2)):
-                block = net.block((net.z + d) % 4, net.x, net.c)
-                piece = self.arrive(it, block)
-                self.copy(it, piece, block, 5 + 2 * n, net.x_peer).start()
-                self.copy(it, piece, block, 6 + 2 * n, net.c_peer).start()
-                pieces.append((piece, block))
-            self.hand_on(it, [self.copy(it, piece, block, 15 + n, net.partner) for n, (piece, block) in enumerate(pieces)])
+            self.total(it, 3, it.z).wait_recv()
+            pieces = self.column(it, net.x, (1, 3, 2))
+            for piece, block in pieces:
+                self.send(it, piece, block, it.x, net.x_peer)
+            self.hand_on(it, pieces, it.y1)
+            for piece, block in pieces:
+                self.send(it, piece, block, it.c, net.c_peer)
 
         self.here(it, body)
 
@@ -472,13 +477,11 @@
         net = self.net
 
         def body():
-            pieces = []
-            for n, d in enumerate((0, 1, 3, 2)):
-                block = net.block((net.z + d) % 4, 1 - net.x, net.c)
-                piece = self.arrive(it, block)
-                self.copy(it, piece, block, 11 + n, net.c_peer).start()
-                pieces.append((piece, block))
-            self.hand_on(it, [self.copy(it, piece, block, 18 + n, net.partner) for n, (piece, block) in enumerate(pieces)])
+            self.total(it, 4, it.x).wait_recv()
+            pieces = self.column(it, 1 - net.x, (0, 1, 3, 2))
+            self.hand_on(it, pieces, it.y2)
+            for piece, block in pieces:
+                self.send(it, piece, block, it.c, net.c_peer)
 
         self.here(it, body)
 
@@ -489,44 +492,34 @@
 
         @pl.when((net.s != it.plane) & (it.plane != 2))
         def _():
-            for n, (d, x) in enumerate(((1, net.x), (3, net.x), (2, net.x), (0, 1 - net.x), (1, 1 - net.x),
-                                        (3, 1 - net.x), (2, 1 - net.x))):
-                block = net.block((net.z + d) % 4, x, net.c)
-                piece = self.arrive(it, block)
-                self.copy(it, piece, block, 5 + n, net.c_peer).start()
+            self.total(it, 3, it.y1).wait_recv()
+            for piece, block in self.column(it, net.x, (1, 3, 2)):
+                self.send(it, piece, block, it.c, net.c_peer)
+            self.total(it, 4, it.y2).wait_recv()
+            for piece, block in self.column(it, 1 - net.x, (0, 1, 3, 2)):
+                self.send(it, piece, block, it.c, net.c_peer)
 
     def from_core(self, it):
-        net = self.net
-
-        @pl.loop(0, 8)
-        def _(n):
-            self.arrive(it, 2 * n + 1 - net.c)
-
+        self.total(it, 8, it.c).wait_recv()
         self.own(it).wait()
 
     def finish(self, it):
         net = self.net
-
-        def sent(first, end):
-            @pl.loop(first, end)
-            def _(k):
-                self.copy(it, it.src, net.f, k, net.c_peer).wait_send()
-
         if isinstance(it.plane, int) and it.plane == 2:
-            sent(0, 15)
+            self.total(it, 15, it.z).wait_send()
             return
 
         @pl.when(it.plane == 2)
         def _():
-            sent(0, 15)
+            self.total(it, 15, it.z).wait_send()
 
         @pl.when(net.s == it.plane)
         def _():
-            sent(0, 22)
+            self.total(it, 22, it.z).wait_send()
 
         @pl.when((net.s != it.plane) & (it.plane != 2))
         def _():
-            sent(4, 12)
+            self.total(it, 8, it.z).wait_send()
 
 
 def full_vector(vec_ref, row, blocks=16, rows=16):
@@ -595,15 +588,18 @@
 N_FC1 = 8
 N_FC2 = 4
 FIRST = 6
+PLANES = (2, 2, 0, 1, 2, 2, 2, 2)
 N_ITEMS = FIRST + N_FC2 + N_FC1
 
 
-def forward_kernel(seg_ref, id_ref, x_ref, vec_ref, qd_ref, pd_ref, pu_ref, wq_hbm, wp_hbm, w1_hbm, w2_hbm,
-                   qu_hbm, g_hbm, u1_hbm, d1_hbm, u2_hbm, d2_hbm,
-                   wqf, wpf, vecf_out, qkv_out, n1_out, c1_out, prob_out, oh_out, att_out, c2_out, gm_out, gr_out, out_out,
-                   wq_own, wq, wp, w1, w2, xp, vecf, qu, g, u1, d1, u2, d2, qkv, n1, c1, qkvw, n1w, c1w, prob, opad, sendb,
-                   oh, att, c2, mid, n2, oacc, gacc, u4, e3, c3, e4, c3t, e4t, act_s, gh_s, gr,
-                   xs_sem, xr_sem, as_sem, ar_sem, loc_sem, out_sem, prob_sem, g_send, g_recv, g_own):
+def block_kernel(seg_ref, id_ref, x_ref, vec_ref, qd_ref, pd_ref, pu_ref, wq_hbm, wp_hbm, w1_hbm, w2_hbm,
+                 qu_hbm, g_hbm, u1_hbm, d1_hbm, u2_hbm, d2_hbm,
+                 vecf_out, prob_out, gm_out, out_out, gall, gn_out,
+                 wq_own, wq, wp, w1, w2, xp, vecf, qu, g, u1, d1, u2, d2, qkv, n1, c1, qkvw, n1w, c1w, prob, opad, sendb,
+                 oh, att, c2, mid, n2, oacc, gacc, u4, e3, c3, e4, c3t, e4t, act_s, gh_s, gr,
+                 do_s, gr_in, gr_sum, last_own, last_in, last_sum, parts0, parts1, parts2, dense0, dense1, dense2, prcv,
+                 xs_sem, xr_sem, as_sem, ar_sem, loc_sem, out_sem, prob_sem, g_sem, g_own,
+                 ds_sem, dr_sem, fs_sem, fr_sem, ps_sem, pr_sem, t_send, t_recv):
     net = Net()
     s, other = net.s, 1 - net.s
     rows, width = x_ref.shape
@@ -626,7 +622,7 @@
         late.append(pltpu.make_async_copy(src, dst, loc_sem.at[6 + n]))
     for copy in pre + late:
         copy.start()
-    net.barrier()
+    net.plane_barrier()
 
     def x_copy(i):
         part = pl.ds(i * chunk, chunk)
@@ -639,8 +635,11 @@
     for copy in pre:
         copy.wait()
 
-    def block(n, src, piece, plane=2):
-        return Block(src, piece, lambda k: g_send.at[n, k], lambda b: g_recv.at[n, b], g_own.at[n], plane)
+    def square(n):
+        return w1.at[pl.ds(0, n * 64), pl.ds(0, half)] if n <= 16 else w1.at[pl.ds(0, n * 32), pl.ds(0, 2 * half)]
+
+    def block(n, src, piece, plane=2, some=square):
+        return Block(src, piece, some, [g_sem.at[k, n] for k in range(N_SEMS)], g_own.at[n], plane)
 
     def wq_part(part):
         cols = pl.ds(part * half, half)
@@ -658,7 +657,8 @@
     def item(n):
         if isinstance(n, int) and n < FIRST:
             if n == 0:
-                return block(0, vec_ref, lambda b: vecf.at[pl.ds(b * 16, 16), :])
+                return block(0, vec_ref, lambda b: vecf.at[pl.ds(b * 16, 16), :], 2,
+                             lambda n: vecf.at[pl.ds(0, n * 16), :])
             return wq_part(n - 1) if n < 4 else wp_part(n - 4)
         if isinstance(n, int):
             return fc2_it(n - FIRST) if n < FIRST + N_FC2 else fc1_it(n - FIRST - N_FC2)
@@ -667,12 +667,12 @@
     def fc2_it(j):
         at = pl.ds(times(j, sub), sub)
         return block(FIRST + j, w2_hbm.at[at, :], lambda b: w2.at[pl.ds(b * fr2 + times(j, sub), sub), :],
-                     (0, 1, 2, 2)[j])
+                     (0, 1, 2, 2)[j], lambda n: w2.at[pl.ds(0, n * sub), :])
 
     def fc1_it(j):
         cols = pl.ds(times(j, FFB), FFB)
         return block(FIRST + N_FC2 + j, w1_hbm.at[:, cols], lambda b: w1.at[pl.ds(b * fr1, fr1), cols],
-                     ((2, 2, 0, 1)[j % 4] if isinstance(j, int) else jnp.where(j % 4 < 2, 2, j % 4 - 2)))
+                     (PLANES[j] if isinstance(j, int) else jnp.where(j // 2 == 1, j % 2, 2)))
 
     gather = Gather(net)
     stages = {"S": gather.start, "A": gather.from_z, "B": gather.from_x, "Y": gather.from_seq, "C": gather.from_core}
@@ -725,7 +725,6 @@
         copy.start()
         outs.append(copy)
 
-    put(wq, wqf)
     put(vecf, vecf_out)
     for src, dst in ((qkv, qkvw), (n1, n1w), (c1, c1w)):
         step = min(src.shape[1], 512)
@@ -734,9 +733,6 @@
         def _(n, src=src, dst=dst, step=step):
             cols = pl.ds(pl.multiple_of(n * step, step), step)
             dst[:, cols] = image.choose(lambda at: src[at:at + WINDOW, cols])
-    put(qkvw, qkv_out)
-    put(n1w, n1_out)
-    put(c1w, c1_out)
     bias = jnp.where(image.inside((1, WINDOW), 1), 0.0, masked_score).astype(F32)
     halves = lane_halves()
 
@@ -749,6 +745,10 @@
         return pltpu.make_async_remote_copy(
             src_ref=sendb.at[pair], dst_ref=att.at[:, cols], send_sem=as_sem.at[pair], recv_sem=ar_sem.at[pair],
             device_id=net.partner, device_id_type=MESH)
+
+    def to_partner(src, dst, send, recv):
+        return pltpu.make_async_remote_copy(src_ref=src, dst_ref=dst, send_sem=send, recv_sem=recv,
+                                            device_id=net.partner, device_id_type=MESH)
 
     pairs = half // 128
 
@@ -798,14 +798,11 @@
         att[:, pl.ds(pl.multiple_of(s * half + pair * 128, 128), 128)] = own_rows(s)
 
     go("B8", "A9", "S12", "S13", "Y6", "Y7")
-    put(wp, wpf)
-    put(oh, oh_out)
 
     @pl.loop(0, pairs)
     def _(pair):
         att_copy(pair).wait_recv()
 
-    put(att, att_out)
     go("A10", "S14")
     bias_p = full_vector(vecf, 2)
     gain2 = full_vector(vecf, 3)
@@ -835,8 +832,7 @@
 
     c3t[...] = c3[...].T
     e4t[...] = e4[...].T
-    put(c2, c2_out)
-    go("B9", "A11", "S15", "C6", "C7", "C8", "C9", "B10", "A12", "A13", "S16", "S17", "B11")
+    go("B9", "A11", "S15", "C6", "C7", "C8", "C9", "B10", "A12", "A13", "S16", "S17")
 
     @pl.loop(0, N_FC1)
     def _(j):
@@ -845,23 +841,13 @@
                                 vecf[pl.ds((2 * j + 1) * 16 + 6, 1), :], vecf[pl.ds((2 * j + 1) * 16 + 7, 1), :]], axis=1)
         col = pl.ds(pl.multiple_of(j * FFB, FFB), FFB)
 
-        @pl.loop(0, 2)
-        def _(i):
-            @pl.when((i == 1) & (j + 4 < N_FC1))
-            def _():
-                gather.from_z(fc1_it(j + 4))
-
-            @pl.when((i == 1) & (j + 2 < N_FC1))
-            def _():
-                gather.from_x(fc1_it(j + 2))
-
-            at = pl.ds(pl.multiple_of(i * chunk, chunk), chunk)
+        for at in [pl.ds(0, rows)]:
             hidden = mm(n2[at, :], w1[:, col]) + mm(c3[at, :], u1[:, col]) + bias
+            grad_active = mm_nt(g[at, :], w2[col, :]) + mm_nt(e4[at, :], d2[col, :])
             cdf = 0.5 * (1.0 + lax.erf(hidden * (0.5 ** 0.5)))
             pdf = jnp.exp(hidden * hidden * -0.5) * (0.5 / 3.141592653589793) ** 0.5
             active = (hidden * cdf).astype(BF16)
             act_s[at, :] = active
-            grad_active = mm_nt(g[at, :], w2[col, :]) + mm_nt(e4[at, :], d2[col, :])
             grad_hidden = (grad_active * (cdf + hidden * pdf)).astype(BF16)
             gh_s[at, :] = grad_hidden
             oacc[at, :] += mm(active, w2[col, :])
@@ -869,14 +855,56 @@
             gacc[at, :] += mm_nt(grad_hidden, w1[:, col])
             e3[at, :] += mm_nt(grad_hidden, u1[:, col])
 
+        @pl.when(j + 4 < N_FC1)
+        def _():
+            gather.from_z(fc1_it(j + 4))
+
+        @pl.when(j == 0)
+        def _():
+            gather.from_x(fc1_it(1))
+
+        @pl.when(j + 2 < N_FC1)
+        def _():
+            gather.from_x(fc1_it(j + 2))
+
         @pl.when(j + 1 < N_FC1)
         def _():
             gather.from_seq(fc1_it(j + 1))
 
         gr[:, col] = compact_rows(mm(c3t[...], gh_s[...]))
         gr[:, pl.ds(pl.multiple_of(ff + j * FFB, FFB), FFB)] = compact_rows(mm(e4t[...], act_s[...]))
+        for first in (0, ff):
+            cols = pl.ds(pl.multiple_of(first + j * FFB, FFB), FFB)
+            to_partner(gr.at[:, cols], gr_in.at[:, cols], fs_sem.at[0], fr_sem.at[0]).start()
 
     bias2 = full_vector(vecf, 5)
+    for n in range(FIRST + N_FC2):
+        gather.finish(item(n))
+
+    @pl.loop(0, N_FC1)
+    def _(j):
+        gather.finish(fc1_it(j))
+
+    for pair in range(pairs - 2, pairs):
+        prob_copy(pair).wait()
+
+    def prob_load(pair):
+        slot = lax.rem(pair, 2)
+        return pltpu.make_async_copy(prob_out.at[pl.ds(2 * pair, 2)], prob.at[slot], prob_sem.at[slot])
+
+    for pair in range(2):
+        prob_load(pair).start()
+
+    g1 = n1
+    e2 = u4
+
+    def grad_att(at, who):
+        heads = pl.ds(pl.multiple_of(who * half, half), half)
+        return (mm_nt(g1[at, :], wp[heads, :]) + mm_nt(e2[at, :].astype(BF16), pd_ref[heads, :])).astype(BF16)
+
+    def d_copy(i):
+        return to_partner(n1.at[pl.ds(rows + i * chunk, chunk), pl.ds(0, half)],
+                          do_s.at[pl.ds(pl.multiple_of(s * rows + i * chunk, chunk), chunk), :], ds_sem.at[i], dr_sem.at[i])
 
     @pl.loop(0, 2)
     def _(i):
@@ -886,230 +914,118 @@
         e = (e3[at, :] * own_select).astype(BF16)
         c3[at, :] = c
         e4[at, :] = e
-        act_out = mid[at, :] + (oacc[at, :] + mm(c, u2[...]) + bias2)
-        xp[at, :] = act_out.astype(BF16)
         grad_n2 = gacc[at, :] + mm_nt(e, d1[...])
-        gacc[at, :] = g[at, :].astype(F32) + norm_grad(mid[at, :], gain2, grad_n2)
-
-    put(xp, out_out)
-    put(gacc, gm_out)
-    gr[:, 2 * ff:2 * ff + width] = compact_rows(mm_tn(e4[...], n2[...]))
-    gr[:, 2 * ff + width:2 * ff + 2 * width] = compact_rows(mm_tn(c3[...], g[...]))
-    put(gr, gr_out)
-    for copy in outs:
-        copy.wait()
-    for pair in range(pairs - 2, pairs):
-        prob_copy(pair).wait()
-    for i in range(2):
-        x_copy(i).wait_send()
-
-    @pl.loop(0, pairs)
-    def _(pair):
-        att_copy(pair).wait_send()
-
-    for n in range(FIRST + N_FC2):
-        gather.finish(item(n))
-
-    @pl.loop(0, N_FC1)
-    def _(j):
-        gather.finish(fc1_it(j))
-
-
-def any_spec():
-    return pl.BlockSpec(memory_space=pl.ANY)
-
-
-def vmem_spec():
-    return pl.BlockSpec(memory_space=pltpu.VMEM)
-
-
-def run_forward(seg, ident, x, vec, qd, pd, pu, wq, wp, w1, w2, qu, g, u1, d1, u2, d2):
-    rows, width = x.shape
-    toks = seg.shape[1]
-    half = width // 2
-    ff = w1.shape[1]
-    dma = pltpu.SemaphoreType.DMA
-    sds = jax.ShapeDtypeStruct
-    gcols = 2 * ff + 2 * width
-    out_shape = (
-        sds((width, 3 * half), BF16), sds((width, width), BF16), sds((256, 128), F32),
-        sds((WINDOW, 3 * half), BF16), sds((WINDOW, width), BF16), sds((WINDOW, 128), BF16),
-        sds((half // 64, WINDOW, WINDOW), BF16), sds((WINDOW, half), BF16), sds((rows, width), BF16), sds((rows, 128), BF16),
-        sds((rows, width), F32), sds((16, gcols), BF16), sds((rows, width), BF16))
-
-    def low(*shape):
-        return pltpu.VMEM(shape, BF16)
-
-    def full(*shape):
-        return pltpu.VMEM(shape, F32)
-
-    scratch = [
-        low(wq.shape[0], 3 * half), low(width, 3 * half), low(width, width), low(width, ff), low(ff, width),
-        low(rows, width), full(256, 128), low(128, 3 * half), low(rows, width), low(128, ff), low(width, 128),
-        low(128, width), low(ff, 128), low(toks, 3 * half), low(toks, width), low(toks, 128),
-        low(WINDOW, 3 * half), low(WINDOW, width), low(WINDOW, 128), low(2, 2, WINDOW, WINDOW), low(2 * PAD + WINDOW, 128),
-        low(half // 128, rows, 128), low(WINDOW, half), low(rows, width), low(rows, 128), full(rows, width), low(rows, width),
-        full(rows, width), full(rows, width), full(rows, 128), full(rows, 128), low(rows, 128), low(rows, 128),
-        low(128, rows), low(128, rows), low(rows, FFB), low(rows, FFB), low(16, gcols),
-        dma((2,)), dma((2,)), dma((4,)), dma((4,)), dma((11,)), dma((12,)), dma((2,)),
-        dma((N_ITEMS, 22)), dma((N_ITEMS, 16)), dma((N_ITEMS,))]
-    return pl.pallas_call(
-        forward_kernel, out_shape=out_shape, in_specs=[vmem_spec()] * 7 + [any_spec()] * 10,
-        out_specs=tuple(any_spec() for unused in out_shape), scratch_shapes=scratch,
-        compiler_params=pltpu.CompilerParams(collective_id=1, has_side_effects=True, vmem_limit_bytes=VMEM_LIMIT),
-        name="forward")(seg, ident, x, vec, qd, pd, pu, wq, wp, w1, w2, qu, g, u1, d1, u2, d2)
-
-
-FIRST_PARTS = 3
-
-
-def adapter_rows(vec_ref):
-    ids = jnp.concatenate([jnp.broadcast_to(vec_ref[16 * p + 8:16 * p + 9, :], (16, 128)) for p in range(16)], axis=0)
-    r = lax.broadcasted_iota(jnp.int32, (256, 128), 0) % 16
-    col = lax.broadcasted_iota(jnp.int32, (256, 128), 1)
-    group = (col // 16).astype(F32)
-    return ((ids == group) & (r == col % 16)).astype(F32).T.astype(BF16)
-
-
-def backward_kernel(seg_ref, id_ref, vec_ref, gm_ref, att_ref, c2_ref, oh_ref, pd_ref, pu_ref, qd_ref, gf_ref, wp_ref,
-                    wq_hbm, qkv_hbm, n1_hbm, c1_hbm, prob_hbm, qu_hbm,
-                    gall, gn_out,
-                    wq, qkv, n1, c1, prob, qu, g1, e2, gsend, do_s, first_own, first_in, last_own, last_in, first_sum, last_sum,
-                    parts1, parts2, dense1, dense2, gq, gpad, psend, prcv, gn,
-                    loc_sem, ds_sem, dr_sem, fs_sem, fr_sem, ps_sem, pr_sem, out_sem, t_send, t_recv, g_send, g_recv, g_own):
-    net = Net()
-    s, other = net.s, 1 - net.s
-    image = Image(seg_ref, id_ref)
-    rows, width = gm_ref.shape
-    half = wq.shape[1] // 3
-    chunk = rows // 2
-    ffn_cols = gf_ref.shape[1]
-    n_first = first_own.shape[1]
-    own1, own2 = n_first // 16, 4 * width // 16
-
-    loads = [pltpu.make_async_copy(src, dst, loc_sem.at[i]) for i, (src, dst) in enumerate(
-        [(qkv_hbm, qkv), (prob_hbm, prob), (wq_hbm, wq), (n1_hbm, n1), (c1_hbm, c1)])]
-    for part in range(3):
-        cols = pl.ds(pl.multiple_of(part * width + s * half, 128), half)
-        loads.append(pltpu.make_async_copy(qu_hbm.at[:, cols], qu.at[:, pl.ds(part * half, half)], loc_sem.at[5 + part]))
-    for copy in loads:
-        copy.start()
-    net.plane_barrier()
-
-    def to_partner(src, dst, send, recv):
-        return pltpu.make_async_remote_copy(src_ref=src, dst_ref=dst, send_sem=send, recv_sem=recv,
-                                            device_id=net.partner, device_id_type=MESH)
+        grad_mid = g[at, :].astype(F32) + norm_grad(mid[at, :], gain2, grad_n2)
+        gacc[at, :] = grad_mid
+        low = grad_mid.astype(BF16)
+        g1[at, :] = low
+        e2[at, :] = mm_nt(low, pu_ref[...]) * own_select
+        n1[pl.ds(pl.multiple_of(rows + i * chunk, chunk), chunk), 0:half] = grad_att(at, other)
+        d_copy(i).start()
+
+    cols0 = 2 * ff
+    cols1 = 4 * width
+    gr[:, cols0:cols0 + width] = compact_rows(mm_tn(e4[...], n2[...]))
+    gr[:, cols0 + width:cols0 + 2 * width] = compact_rows(mm_tn(c3[...], g[...]))
+    gr[:, cols0 + 2 * width:cols0 + 3 * width] = compact_rows(mm_tn(c2[...], g1[0:rows, :]))
+    gr[:, cols0 + 3 * width:cols0 + 4 * width] = compact_rows(mm_tn(e2[...].astype(BF16), att[...]))
+    rest = pl.ds(cols0, cols1)
+    rest_copy = to_partner(gr.at[:, rest], gr_in.at[:, rest], fs_sem.at[1], fr_sem.at[1])
+    rest_copy.start()
 
     @pl.loop(0, 2)
     def _(i):
         at = pl.ds(pl.multiple_of(i * chunk, chunk), chunk)
-        low = gm_ref[at, :].astype(BF16)
-        g1[at, :] = low
-        e2[at, :] = mm_nt(low, pu_ref[...]) * image.select(s * rows + i * chunk, chunk)
-
-    def grad_att(i, who):
-        at = pl.ds(i * chunk, chunk)
-        heads = pl.ds(pl.multiple_of(who * half, half), half)
-        return (mm_nt(g1[at, :], wp_ref[heads, :]) + mm_nt(e2[at, :].astype(BF16), pd_ref[heads, :])).astype(BF16)
-
-    dsend = []
-    for i in range(2):
-        gsend[i] = grad_att(i, other)
-        copy = to_partner(gsend.at[i], do_s.at[pl.ds(pl.multiple_of(s * rows + i * chunk, chunk), chunk), :],
-                          ds_sem.at[i], dr_sem.at[i])
-        copy.start()
-        dsend.append(copy)
-    first_own[:, 0:ffn_cols] = gf_ref[...]
-    first_own[:, ffn_cols:ffn_cols + width] = compact_rows(mm_tn(c2_ref[...], g1[...]))
-    first_own[:, ffn_cols + width:ffn_cols + 2 * width] = compact_rows(mm_tn(e2[...].astype(BF16), att_ref[...]))
-    fsend = to_partner(first_own, first_in, fs_sem.at[0], fr_sem.at[0])
-    fsend.start()
-    for i in range(2):
-        do_s[pl.ds(pl.multiple_of(s * rows + i * chunk, chunk), chunk), :] = grad_att(i, s)
-    zeros = jnp.zeros((PAD, width), F32)
-    gpad[0:PAD, :] = zeros
-    gpad[PAD + WINDOW:2 * PAD + WINDOW, :] = zeros
-    last_own[...] = jnp.zeros_like(last_own)
-    pick = adapter_rows(vec_ref)
-
-    def turn(n, src, dst, cols, d):
-        peer = (net.f + d) % 16
-        return pltpu.make_async_remote_copy(
-            src_ref=src.at[:, pl.ds(pl.multiple_of(peer * cols, 128), cols)],
-            dst_ref=dst.at[pl.ds(pl.multiple_of(net.f * 16, 16), 16), :], send_sem=t_send.at[n, d],
-            recv_sem=t_recv.at[n, net.f], device_id={"fsdp": peer}, device_id_type=MESH)
-
-    def turn_start(n, src, dst, cols):
-        @pl.loop(1, 16)
-        def _(d):
-            turn(n, src, dst, cols, d).start()
-
-        dst[pl.ds(pl.multiple_of(net.f * 16, 16), 16), :] = src[:, pl.ds(pl.multiple_of(net.f * cols, 128), cols)]
-
-    def turn_wait(n, src, dst, cols):
+        do_s[pl.ds(pl.multiple_of(s * rows + i * chunk, chunk), chunk), :] = grad_att(at, s)
+
+    own0, own1 = cols0 // 16, cols1 // 16
+    pick = adapter_rows(vecf)
+
+    def turn_start(n, src, first, dst, cols):
+        mine = pl.ds(pl.multiple_of(net.f * 16, 16), 16)
+
         @pl.loop(1, 16)
         def _(d):
             peer = (net.f + d) % 16
             pltpu.make_async_remote_copy(
-                src_ref=src.at[:, pl.ds(0, cols)], dst_ref=dst.at[pl.ds(pl.multiple_of(peer * 16, 16), 16), :],
-                send_sem=t_send.at[n, d], recv_sem=t_recv.at[n, peer], device_id={"fsdp": peer},
-                device_id_type=MESH).wait_recv()
-
-    def turn_finish(n, src, dst, cols):
-        @pl.loop(1, 16)
-        def _(d):
-            turn(n, src, dst, cols, d).wait_send()
-
-    def block(n, src, first, step, cols):
-        return Block(src, lambda b: gall.at[:, pl.ds(pl.multiple_of(first + b * step, 128), cols)],
-                     lambda k: g_send.at[n, k], lambda b: g_recv.at[n, b], g_own.at[n])
-
-    share = own1 // FIRST_PARTS
-    items = [block(n, dense1.at[:, pl.ds(n * share, share)], n * share, own1, share) for n in range(FIRST_PARTS)]
-    items.append(block(FIRST_PARTS, dense2, n_first, own2, own2))
-    gather = Gather(net)
-    stages = {"S": gather.start, "A": gather.from_z, "B": gather.from_x, "C": gather.from_core}
-
-    def go(*steps):
+                src_ref=src.at[:, pl.ds(pl.multiple_of(first + peer * cols, 128), cols)], dst_ref=dst.at[mine, :],
+                send_sem=t_send.at[n], recv_sem=t_recv.at[n], device_id={"fsdp": peer}, device_id_type=MESH).start()
+
+        dst[mine, :] = src[:, pl.ds(pl.multiple_of(first + net.f * cols, 128), cols)]
+
+    def turn_total(n, dst):
+        return pltpu.make_async_remote_copy(
+            src_ref=dst.at[0:240, :], dst_ref=dst.at[0:240, :], send_sem=t_send.at[n], recv_sem=t_recv.at[n],
+            device_id=net.c_peer, device_id_type=MESH)
+
+    def result(n, src, first, step):
+        return Block(src, lambda b: gall.at[:, pl.ds(pl.multiple_of(first + b * step, 128), 256)],
+                     lambda m: gall.at[:, pl.ds(0, m * 256)], [g_sem.at[k, N_ITEMS + n] for k in range(N_SEMS)],
+                     g_own.at[N_ITEMS + n])
+
+    results = [result(0, dense0.at[:, pl.ds(0, 256)], 0, own0), result(1, dense0.at[:, pl.ds(256, 256)], 256, own0),
+               result(2, dense1, cols0, own1), result(3, dense2, cols0 + cols1, own1)]
+
+    def move(*steps):
         for step in steps:
-            stages[step[0]](items[int(step[1:])])
-
-    for copy in loads:
-        copy.wait()
-    for copy in dsend:
-        copy.wait_recv()
-
-    halves = lane_halves()
+            stages[step[0]](results[int(step[1:])])
+
+    first_cols = pl.ds(0, cols0)
+    first_copy = to_partner(gr.at[:, first_cols], gr_in.at[:, first_cols], fs_sem.at[0], fr_sem.at[0])
+    first_copy.wait_recv()
+    gr_sum[:, 0:cols0] = (gr[:, 0:cols0].astype(F32) + gr_in[:, 0:cols0].astype(F32)).astype(BF16)
+    turn_start(0, gr_sum, 0, parts0, own0)
+
+    @pl.loop(0, 2)
+    def _(i):
+        at = pl.ds(pl.multiple_of(i * chunk, chunk), chunk)
+        branch = oacc[at, :] + mm(c3[at, :], u2[...]) + bias2
+        xp[at, :] = (mid[at, :] + branch).astype(BF16)
+
+    put(xp, out_out)
+    put(gacc, gm_out)
+    gpad = w2
+    zeros = jnp.zeros((PAD, width), BF16)
+    gpad[0:PAD, :] = zeros
+    gpad[PAD + WINDOW:2 * PAD + WINDOW, :] = zeros
+    last_own[...] = jnp.zeros_like(last_own)
+    turn_total(0, parts0).wait_recv()
+    dense0[...] = mm(pick, parts0[...]).astype(BF16)
+    move("S0", "S1")
+    for i in range(2):
+        d_copy(i).wait_recv()
+
+    gq = w1
     scale = HEAD_DIM ** (-0.5)
     keep = image.inside((WINDOW, 1), 0).astype(BF16)
 
-    @pl.loop(0, half // 128)
+    @pl.loop(0, pairs)
     def _(pair):
-        @pl.when(pair == 1)
+        @pl.when(pair == 2)
         def _():
-            fsend.wait_recv()
-            first_sum[...] = (first_own[...].astype(F32) + first_in[...].astype(F32)).astype(BF16)
-            turn_start(0, first_sum, parts1, own1)
+            rest_copy.wait_recv()
+            gr_sum[:, cols0:cols0 + cols1] = (gr[:, cols0:cols0 + cols1].astype(F32)
+                                              + gr_in[:, cols0:cols0 + cols1].astype(F32)).astype(BF16)
+            turn_start(1, gr_sum, cols0, parts1, own1)
 
         @pl.when(pair == 3)
         def _():
-            turn_wait(0, first_sum, parts1, own1)
-            for n in range(FIRST_PARTS):
-                dense1[:, n * share:(n + 1) * share] = mm(pick, parts1[:, n * share:(n + 1) * share]).astype(BF16)
-            go("S0", "S1", "S2")
+            move("A0")
 
         def cols(part):
             return pl.ds(pl.multiple_of(part * half + pair * 128, 128), 128)
 
-        k2 = qkv[:, cols(1)]
-        v2 = qkv[:, cols(2)]
-        q2 = qkv[:, cols(0)] * jnp.asarray(scale, BF16)
+        prob_load(pair).wait()
+        slot = lax.rem(pair, 2)
+        k2 = qkvw[:, cols(1)]
+        v2 = qkvw[:, cols(2)]
+        q2 = qkvw[:, cols(0)] * jnp.asarray(scale, BF16)
         do2 = image.choose(lambda at: do_s[at:at + WINDOW, cols(0)]) * keep
-        inner = do2.astype(F32) * oh_ref[:, cols(0)].astype(F32)
+        inner = do2.astype(F32) * oh[:, cols(0)].astype(F32)
         gv = gk = gqq = None
         for hd in range(2):
             hm = halves[hd].astype(BF16)
-            weights = prob[2 * pair + hd]
+            weights = prob[slot, hd]
             grad_p = mm_nt(do2 * hm, v2)
             row_inner = jnp.sum(inner * halves[hd], axis=1, keepdims=True)
             grad_s = (weights.astype(F32) * (grad_p - row_inner)).astype(BF16)
@@ -1119,86 +1035,131 @@
             gv = dv if gv is None else gv + dv
             gk = dk if gk is None else gk + dk
             gqq = dq if gqq is None else gqq + dq
-        gq[:, cols(0)] = (gqq * scale).astype(BF16)
-        gq[:, cols(1)] = gk.astype(BF16)
-        gq[:, cols(2)] = gv.astype(BF16)
-
-    up = compact_rows(mm_tn(c1[...], gq[...]))
-    e1 = (mm_nt(gq[...], qu[...]) * image.select_window(0, WINDOW)).astype(BF16)
+
+        @pl.when(pair + 2 < pairs)
+        def _():
+            prob_load(pair + 2).start()
+
+        gq[0:WINDOW, cols(0)] = (gqq * scale).astype(BF16)
+        gq[0:WINDOW, cols(1)] = gk.astype(BF16)
+        gq[0:WINDOW, cols(2)] = gv.astype(BF16)
+
+    three = slice(0, 3 * half)
+    c1[0:WINDOW, :] = (mm_nt(gq[0:WINDOW, three], qu[...]) * image.select_window(0, WINDOW)).astype(BF16)
+    up = compact_rows(mm_tn(c1w[...], gq[0:WINDOW, three]))
     for part in range(3):
         last_own[:, pl.ds(pl.multiple_of(part * width + s * half, 128), half)] = up[:, part * half:(part + 1) * half]
-    last_own[:, 3 * width:4 * width] = compact_rows(mm_tn(e1, n1[...]))
-    lsend = to_partner(last_own, last_in, fs_sem.at[1], fr_sem.at[1])
-    lsend.start()
+    last_own[:, 3 * width:4 * width] = compact_rows(mm_tn(c1[0:WINDOW, :], n1w[...]))
+    last_copy = to_partner(last_own, last_in, fs_sem.at[2], fr_sem.at[2])
+    last_copy.start()
+    move("A1")
 
     @pl.loop(0, 2)
     def _(i):
         at = pl.ds(pl.multiple_of(i * QROWS, QROWS), QROWS)
-        e1_rows = (mm_nt(gq[at, :], qu[...]) * image.select_window(i * QROWS, QROWS)).astype(BF16)
-        gpad[pl.ds(pl.multiple_of(PAD + i * QROWS, STEP), QROWS), :] = mm_nt(gq[at, :], wq[...]) + mm_nt(e1_rows, qd_ref[...])
+        gpad[pl.ds(pl.multiple_of(PAD + i * QROWS, STEP), QROWS), :] = (
+            mm_nt(gq[at, three], wq[...]) + mm_nt(c1[at, :], qd_ref[...])).astype(BF16)
 
     def rows_of(who, i):
         return image.choose(lambda at: gpad[pl.ds(pl.multiple_of(who * rows + PAD + i * chunk - at, STEP), chunk), :])
 
-    psends = []
+    spot = 2 * PAD + WINDOW + 128
+
+    def p_copy(i):
+        return to_partner(gpad.at[pl.ds(spot + i * chunk, chunk), :], prcv.at[i], ps_sem.at[i], pr_sem.at[i])
+
     for i in range(2):
-        psend[i] = rows_of(other, i).astype(BF16)
-        copy = to_partner(psend.at[i], prcv.at[i], ps_sem.at[i], pr_sem.at[i])
-        copy.start()
-        psends.append(copy)
-    go("A0")
-    lsend.wait_recv()
+        gpad[spot + i * chunk:spot + (i + 1) * chunk, :] = rows_of(other, i)
+        p_copy(i).start()
+    last_copy.wait_recv()
     last_sum[...] = (last_own[...].astype(F32) + last_in[...].astype(F32)).astype(BF16)
-    turn_start(1, last_sum, parts2, own2)
-    go("A1", "B0", "A2", "B1")
-    turn_wait(1, last_sum, parts2, own2)
+    turn_start(2, last_sum, 0, parts2, own1)
+    turn_total(1, parts1).wait_recv()
+    dense1[...] = mm(pick, parts1[...]).astype(BF16)
+    move("B0", "S2", "B1")
+    turn_total(2, parts2).wait_recv()
     dense2[...] = mm(pick, parts2[...]).astype(BF16)
-    go("S3", "B2", "C0", "C1", "A3", "C2", "B3")
-    outs = []
+    move("S3", "C0", "A2", "C1", "A3", "B2", "C2", "B3")
+    gn = oacc
     for i in range(2):
-        psends[i].wait_recv()
-        rows_at = pl.ds(i * chunk, chunk)
-        gn[rows_at, :] = prcv[i].astype(F32) + rows_of(s, i)
-        copy = pltpu.make_async_copy(gn.at[rows_at, :], gn_out.at[rows_at, :], out_sem.at[i])
-        copy.start()
-        outs.append(copy)
-    go("C3")
+        p_copy(i).wait_recv()
+        at = slice(i * chunk, (i + 1) * chunk)
+        gn[at, :] = prcv[i].astype(F32) + rows_of(s, i).astype(F32)
+        put(gn.at[at, :], gn_out.at[at, :])
+    move("C3")
     for copy in outs:
         copy.wait()
-    for copy in dsend + [fsend, lsend] + psends:
+    for i in range(2):
+        x_copy(i).wait_send()
+        d_copy(i).wait_send()
+        p_copy(i).wait_send()
+    for copy in (first_copy, rest_copy, last_copy):
         copy.wait_send()
-    turn_finish(0, first_sum, parts1, own1)
-    turn_finish(1, last_sum, parts2, own2)
-    for it in items:
+    for n, dst in enumerate((parts0, parts1, parts2)):
+        turn_total(n, dst).wait_send()
+    for it in results:
         gather.finish(it)
 
-
-def run_backward(seg, ident, vec, gm, att, c2, oh, pd, pu, qd, gf, wp, wq, qkv, n1, c1, prob, qu):
-    rows, width = gm.shape
-    toks = 2 * rows
+    @pl.loop(0, pairs)
+    def _(pair):
+        att_copy(pair).wait_send()
+
+
+def any_spec():
+    return pl.BlockSpec(memory_space=pl.ANY)
+
+
+def vmem_spec():
+    return pl.BlockSpec(memory_space=pltpu.VMEM)
+
+
+def adapter_rows(vec_ref):
+    ids = jnp.concatenate([jnp.broadcast_to(vec_ref[16 * p + 8:16 * p + 9, :], (16, 128)) for p in range(16)], axis=0)
+    r = lax.broadcasted_iota(jnp.int32, (256, 128), 0) % 16
+    col = lax.broadcasted_iota(jnp.int32, (256, 128), 1)
+    group = (col // 16).astype(F32)
+    return ((ids == group) & (r == col % 16)).astype(F32).T.astype(BF16)
+
+
+def run_block(seg, ident, x, vec, qd, pd, pu, wq, wp, w1, w2, qu, g, u1, d1, u2, d2):
+    rows, width = x.shape
+    toks = seg.shape[1]
     half = width // 2
+    ff = w1.shape[1]
+    chunk = rows // 2
     dma = pltpu.SemaphoreType.DMA
     sds = jax.ShapeDtypeStruct
-    n_first = gf.shape[1] + 2 * width
-    out_shape = (sds((128, n_first + 4 * width), BF16), sds((rows, width), F32))
-    chunk = rows // 2
+    gcols = 2 * ff + 4 * width
+    last = 4 * width
+    out_shape = (
+        sds((256, 128), F32), sds((half // 64, WINDOW, WINDOW), BF16), sds((rows, width), F32), sds((rows, width), BF16),
+        sds((128, gcols + last), BF16), sds((rows, width), F32))
 
     def low(*shape):
         return pltpu.VMEM(shape, BF16)
 
+    def full(*shape):
+        return pltpu.VMEM(shape, F32)
+
     scratch = [
-        low(*wq.shape), low(*qkv.shape), low(*n1.shape), low(*c1.shape), low(*prob.shape), low(128, 3 * half), low(rows, width),
-        pltpu.VMEM((rows, 128), F32), low(2, chunk, half), low(toks, half), low(16, n_first), low(16, n_first),
-        low(16, 4 * width), low(16, 4 * width), low(16, n_first), low(16, 4 * width), low(256, n_first // 16),
-        low(256, width // 4), low(128, n_first // 16), low(128, width // 4), low(WINDOW, 3 * half),
-        pltpu.VMEM((2 * PAD + WINDOW, width), F32), low(2, chunk, width), low(2, chunk, width), pltpu.VMEM((rows, width), F32),
-        dma((8,)), dma((2,)), dma((2,)), dma((2,)), dma((2,)), dma((2,)), dma((2,)), dma((2,)), dma((2, 16)), dma((2, 16)),
-        dma((FIRST_PARTS + 1, 22)), dma((FIRST_PARTS + 1, 16)), dma((FIRST_PARTS + 1,))]
+        low(wq.shape[0], 3 * half), low(width, 3 * half), low(width, width), low(width, ff), low(ff, width),
+        low(rows, width), full(256, 128), low(128, 3 * half), low(rows, width), low(128, ff), low(width, 128),
+        low(128, width), low(ff, 128), low(toks, 3 * half), low(toks, width), low(toks, 128),
+        low(WINDOW, 3 * half), low(WINDOW, width), low(WINDOW, 128), low(2, 2, WINDOW, WINDOW), low(2 * PAD + WINDOW, 128),
+        low(half // 128, rows, 128), low(WINDOW, half), low(rows, width), low(rows, 128), full(rows, width), low(rows, width),
+        full(rows, width), full(rows, width), full(rows, 128), full(rows, 128), low(rows, 128), low(rows, 128),
+        low(128, rows), low(128, rows), low(rows, FFB), low(rows, FFB), low(16, gcols),
+        low(toks, half), low(16, gcols), low(16, gcols), low(16, last), low(16, last), low(16, last),
+        low(256, 2 * ff // 16), low(256, last // 16), low(256, last // 16), low(128, 2 * ff // 16), low(128, last // 16),
+        low(128, last // 16), low(2, chunk, width),
+        dma((2,)), dma((2,)), dma((4,)), dma((4,)), dma((11,)), dma((12,)), dma((2,)),
+        dma((N_SEMS, N_ITEMS + 4)), dma((N_ITEMS + 4,)),
+        dma((2,)), dma((2,)), dma((3,)), dma((3,)), dma((2,)), dma((2,)), dma((3,)), dma((3,))]
     return pl.pallas_call(
-        backward_kernel, out_shape=out_shape, in_specs=[vmem_spec()] * 12 + [any_spec()] * 6,
+        block_kernel, out_shape=out_shape, in_specs=[vmem_spec()] * 7 + [any_spec()] * 10,
         out_specs=tuple(any_spec() for unused in out_shape), scratch_shapes=scratch,
-        compiler_params=pltpu.CompilerParams(collective_id=2, has_side_effects=True, vmem_limit_bytes=VMEM_LIMIT),
-        name="backward")(seg, ident, vec, gm, att, c2, oh, pd, pu, qd, gf, wp, wq, qkv, n1, c1, prob, qu)
+        compiler_params=pltpu.CompilerParams(collective_id=1, has_side_effects=True, vmem_limit_bytes=VMEM_LIMIT),
+        name="block")(seg, ident, x, vec, qd, pd, pu, wq, wp, w1, w2, qu, g, u1, d1, u2, d2)
 
 
 def expand_kernel(vec_ref, f1u, f2d, f1d, f2u, pu, pdn, qu, qd, gn, x, gm,
@@ -1250,10 +1211,9 @@
     vec = jnp.concatenate([
         jnp.concatenate([six * (1.0 - odd), six * odd], axis=1), fc1_bias.astype(F32).reshape(2, 128),
         jnp.broadcast_to(adapter_ids[0].astype(F32)[:, None], (1, 128)), jnp.zeros((7, 128), F32)], axis=0)
-    (wq, wp, vecf, qkv, n1, c1, prob, oh, att, c2, gm, gf, out) = run_forward(
+    vecf, unused, gm, out, gall, gn = run_block(
         segments, adapter_ids, x, vec, qkv_down, proj_down, proj_up, w_qkv, w_proj, w_fc1, w_fc2, qkv_up,
         grad_out[0], fc1_up, fc1_down, fc2_up, fc2_down)
-    gall, gn = run_backward(segments, adapter_ids, vecf, gm, att, c2, oh, proj_down, proj_up, qkv_down, gf, wp, wq, qkv, n1, c1, prob, qkv_up)
     gt, gqd, gqu, gpd, gpu, gf1d, gf1u, gf2d, gf2u = run_expand(vecf, gall, gn, x, gm)
     return out[None], gt[None], gqd, gqu, gpd, gpu, gf1d, gf1u, gf2d, gf2u
 

time: 239 us -> 207 us (0.87)
  Pallas kernels: 234 us -> 200 us
    pallas_call x2 -> x1, Pallas kernels: 225 us -> 191 us  [run_block(): pl.pallas_call(block_kernel, out_shape=out_shape, in_specs=[vmem_spec()]...]
where the time goes in v2:
time: 207 us; the launch traced here: 206 us
  Pallas kernels  200 us (97%)
  local copies, waits for them, and re-layouts  3.18 us (2%)
    pallas_call x1, Pallas kernels, run_block(): pl.pallas_call(block_kernel, out_shape=out_shape, in_specs=[vmem_spec()]...  191 us
    pallas_call x1, Pallas kernels, run_expand(): pl.pallas_call(expand_kernel, grid=(n,), out_shape=(sds((rows, width), F3...  8.52 us

profile of v2, /device:TPU:11, one launch (start us, length us, event | category | flops | bytes accessed | tf_op | source)
XLA Modules:
  0.0 205.8 jit_solution(7938993581219381653)
XLA Ops:
  1.3 0.1 pad.3.clone
  1.4 0.1 pad.4.clone
  1.5 0.7 bitcast_convert_fusion
  2.1 0.8 stack.27
  2.9 0.7 maximum_maximum_fusion.vec_ref
  3.6 191.4 %block.1 = (f32[256,128]{1,0:T(8,128)}, bf16[8,640,640]{2,1,0:T(8,128)(2,1)}, f32[512,1024]{1,0:T(8,128)}, bf16[512,1024]{1,0:T(8,128)(2,1)}, bf16[128,16384]{1,0:T(8,128)(2,1)}, /*index=5*/f32[512,1024]{1,0:T(8,128)}) custom-call(s32[1,1024]{1,0:T(1,128)} %seg_ref.1, s32[1,1]{1,0:T(1,128)S(6)} %copy.34.id_ref, bf16[512,1024]{1,0:T(8,128)(2,1)} %bitcast.16, ...), custom_call_target="tpu_custom_call" | custom-call | tf_op jit(solution)/shard_map/block/pallas_call | solution.py:1158
  195.0 8.5 %expand.1 = (f32[512,1024]{1,0:T(8,128)}, f32[1024,128]{1,0:T(8,128)}, f32[128,3072]{1,0:T(8,128)}, f32[1024,128]{1,0:T(8,128)}, f32[128,1024]{1,0:T(8,128)}, /*...) custom-call(f32[256,128]{1,0:T(8,128)} %get-tuple-element.25.vec_ref, ...), custom_call_target="tpu_custom_call" | custom-call | tf_op jit(solution)/shard_map/expand/pallas_call | solution.py:1191
  203.5 2.3 %copy.35 = bf16[1,512,1024]{2,1,0:T(8,128)(2,1)} copy(bf16[1,512,1024]{2,1,0:T(8,128)(2,1)} %bitcast.19) | data formatting | bytes 2097152
  (2 shorter events, 0.0 us)

commit v3 on v2

--- a/solution.py
+++ b/solution.py
@@ -686,7 +686,7 @@
     zeros = jnp.zeros((PAD, 128), BF16)
     opad[0:PAD, :] = zeros
     opad[PAD + WINDOW:2 * PAD + WINDOW, :] = zeros
-    go("A0", "A1", "S3", "A2", "S4", "S5", "B0", "B1", "A3", "S6", "S7", "B2", "A4", "A5", "S8")
+    go("A0", "A1", "S3", "A2", "S4", "S5", "B0", "B1", "A3", "S6", "S7", "B2")
     for copy in late:
         copy.wait()
     go("B3", "C0", "C1", "C2", "C3")
@@ -714,6 +714,7 @@
         project(xp, i * chunk, pl.multiple_of(other * rows + i * chunk, chunk))
 
     own_rows_in(0)
+    go("A4", "A5", "S8")
     own_rows_in(1)
     partner_rows_in(0)
     partner_rows_in(1)
@@ -757,7 +758,7 @@
         def cols(part):
             return pl.ds(pl.multiple_of(part * half + pair * 128, 128), 128)
 
-        for n, steps in enumerate(((), ("Y4", "Y5"), ("B6", "B7", "A8", "S10", "S11"), ("C4", "C5"))):
+        for n, steps in enumerate(((), ("Y4", "Y5"), ("A8", "S10", "S11"), ("C4", "C5"))):
             @pl.when(pair == n)
             def _(steps=steps):
                 go(*steps)
@@ -797,13 +798,13 @@
         att_copy(pair).start()
         att[:, pl.ds(pl.multiple_of(s * half + pair * 128, 128), 128)] = own_rows(s)
 
-    go("B8", "A9", "S12", "S13", "Y6", "Y7")
+    go("B6", "B7")
 
     @pl.loop(0, pairs)
     def _(pair):
         att_copy(pair).wait_recv()
 
-    go("A10", "S14")
+    go("A9", "S12", "S13")
     bias_p = full_vector(vecf, 2)
     gain2 = full_vector(vecf, 3)
     shift2 = full_vector(vecf, 4)
@@ -832,7 +833,7 @@
 
     c3t[...] = c3[...].T
     e4t[...] = e4[...].T
-    go("B9", "A11", "S15", "C6", "C7", "C8", "C9", "B10", "A12", "A13", "S16", "S17")
+    go("B8", "A10", "S14", "Y6", "Y7", "B9", "A11", "S15", "C6", "C7", "C8", "C9", "B10", "A12", "A13", "S16", "S17")
 
     @pl.loop(0, N_FC1)
     def _(j):
@@ -902,9 +903,10 @@
         heads = pl.ds(pl.multiple_of(who * half, half), half)
         return (mm_nt(g1[at, :], wp[heads, :]) + mm_nt(e2[at, :].astype(BF16), pd_ref[heads, :])).astype(BF16)
 
-    def d_copy(i):
-        return to_partner(n1.at[pl.ds(rows + i * chunk, chunk), pl.ds(0, half)],
-                          do_s.at[pl.ds(pl.multiple_of(s * rows + i * chunk, chunk), chunk), :], ds_sem.at[i], dr_sem.at[i])
+    def d_copy(pair):
+        cols = pl.ds(pair * 128 if isinstance(pair, int) else pl.multiple_of(pair * 128, 128), 128)
+        return to_partner(n1.at[pl.ds(rows, rows), cols],
+                          do_s.at[pl.ds(pl.multiple_of(s * rows, rows), rows), cols], ds_sem.at[pair], dr_sem.at[pair])
 
     @pl.loop(0, 2)
     def _(i):
@@ -921,7 +923,9 @@
         g1[at, :] = low
         e2[at, :] = mm_nt(low, pu_ref[...]) * own_select
         n1[pl.ds(pl.multiple_of(rows + i * chunk, chunk), chunk), 0:half] = grad_att(at, other)
-        d_copy(i).start()
+
+    for pair in range(pairs):
+        d_copy(pair).start()
 
     cols0 = 2 * ff
     cols1 = 4 * width
@@ -989,33 +993,30 @@
     gpad[0:PAD, :] = zeros
     gpad[PAD + WINDOW:2 * PAD + WINDOW, :] = zeros
     last_own[...] = jnp.zeros_like(last_own)
-    turn_total(0, parts0).wait_recv()
-    dense0[...] = mm(pick, parts0[...]).astype(BF16)
-    move("S0", "S1")
-    for i in range(2):
-        d_copy(i).wait_recv()
-
     gq = w1
     scale = HEAD_DIM ** (-0.5)
     keep = image.inside((WINDOW, 1), 0).astype(BF16)
 
     @pl.loop(0, pairs)
     def _(pair):
-        @pl.when(pair == 2)
+        @pl.when(pair == 1)
+        def _():
+            turn_total(0, parts0).wait_recv()
+            dense0[...] = mm(pick, parts0[...]).astype(BF16)
+            move("S0", "S1")
+
+        @pl.when(pair == 3)
         def _():
             rest_copy.wait_recv()
             gr_sum[:, cols0:cols0 + cols1] = (gr[:, cols0:cols0 + cols1].astype(F32)
                                               + gr_in[:, cols0:cols0 + cols1].astype(F32)).astype(BF16)
             turn_start(1, gr_sum, cols0, parts1, own1)
 
-        @pl.when(pair == 3)
-        def _():
-            move("A0")
-
         def cols(part):
             return pl.ds(pl.multiple_of(part * half + pair * 128, 128), 128)
 
         prob_load(pair).wait()
+        d_copy(pair).wait_recv()
         slot = lax.rem(pair, 2)
         k2 = qkvw[:, cols(1)]
         v2 = qkvw[:, cols(2)]
@@ -1052,7 +1053,7 @@
     last_own[:, 3 * width:4 * width] = compact_rows(mm_tn(c1[0:WINDOW, :], n1w[...]))
     last_copy = to_partner(last_own, last_in, fs_sem.at[2], fr_sem.at[2])
     last_copy.start()
-    move("A1")
+    move("A0", "A1")
 
     @pl.loop(0, 2)
     def _(i):
@@ -1091,7 +1092,6 @@
         copy.wait()
     for i in range(2):
         x_copy(i).wait_send()
-        d_copy(i).wait_send()
         p_copy(i).wait_send()
     for copy in (first_copy, rest_copy, last_copy):
         copy.wait_send()
@@ -1103,6 +1103,7 @@
     @pl.loop(0, pairs)
     def _(pair):
         att_copy(pair).wait_send()
+        d_copy(pair).wait_send()
 
 
 def any_spec():
@@ -1154,7 +1155,7 @@
         low(128, last // 16), low(2, chunk, width),
         dma((2,)), dma((2,)), dma((4,)), dma((4,)), dma((11,)), dma((12,)), dma((2,)),
         dma((N_SEMS, N_ITEMS + 4)), dma((N_ITEMS + 4,)),
-        dma((2,)), dma((2,)), dma((3,)), dma((3,)), dma((2,)), dma((2,)), dma((3,)), dma((3,))]
+        dma((4,)), dma((4,)), dma((3,)), dma((3,)), dma((2,)), dma((2,)), dma((3,)), dma((3,))]
     return pl.pallas_call(
         block_kernel, out_shape=out_shape, in_specs=[vmem_spec()] * 7 + [any_spec()] * 10,
         out_specs=tuple(any_spec() for unused in out_shape), scratch_shapes=scratch,
@@ -1162,20 +1163,21 @@
         name="block")(seg, ident, x, vec, qd, pd, pu, wq, wp, w1, w2, qu, g, u1, d1, u2, d2)
 
 
-def expand_kernel(vec_ref, f1u, f2d, f1d, f2u, pu, pdn, qu, qd, gn, x, gm,
-                  gt_out, qd_out, qu_out, pd_out, pu_out, f1d_out, f1u_out, f2d_out, f2u_out):
+def expand_kernel(vec_ref, f1u, f2d, f1d, f2u, pu, pdn, qu, qd, gn, x, gm, out,
+                  out_out, gt_out, qd_out, qu_out, pd_out, pu_out, f1d_out, f1u_out, f2d_out, f2u_out):
     for src, dst in ((f1u, f1u_out), (f2u, f2u_out), (pu, pu_out), (qu, qu_out)):
         dst[...] = src[...].astype(F32)
     for src, dst in ((f1d, f1d_out), (f2d, f2d_out), (pdn, pd_out), (qd, qd_out)):
-        dst[...] = src[...].astype(F32).T
+        dst[...] = src[...].T.astype(F32)
+    out_out[...] = out[...]
     gain1 = full_vector(vec_ref, 0)
     gt_out[...] = gm[...] + norm_grad(x[...].astype(F32), gain1, gn[...])
 
 
-def run_expand(vec, gall, gn, x, gm):
+def run_expand(vec, gall, gn, x, gm, out):
     rows, width = gn.shape
     ff = 4 * width
-    n = 4
+    n = 2
     sds = jax.ShapeDtypeStruct
 
     def part(cols, offset):
@@ -1190,16 +1192,16 @@
     q = width // n
     return pl.pallas_call(
         expand_kernel, grid=(n,),
-        out_shape=(sds((rows, width), F32), sds((width, 128), F32), sds((128, 3 * width), F32), sds((width, 128), F32),
+        out_shape=(sds((rows, width), BF16), sds((rows, width), F32), sds((width, 128), F32), sds((128, 3 * width), F32), sds((width, 128), F32),
                    sds((128, width), F32), sds((width, 128), F32), sds((128, ff), F32), sds((ff, 128), F32), sds((128, width), F32)),
         in_specs=[pl.BlockSpec((256, 128), lambda j: (0, 0)), part(ff // n, 0), part(ff // n, ff), part(q, 2 * ff),
                   part(q, 2 * ff + width), part(q, 2 * ff + 2 * width), part(q, 2 * ff + 3 * width),
                   part(3 * q, 2 * ff + 4 * width), part(q, 2 * ff + 7 * width),
-                  by_row((rows // n, width)), by_row((rows // n, width)), by_row((rows // n, width))],
-        out_specs=(by_row((rows // n, width)), by_row((q, 128)), by_col((128, 3 * q)), by_row((q, 128)), by_col((128, q)),
+                  by_row((rows // n, width)), by_row((rows // n, width)), by_row((rows // n, width)), by_row((rows // n, width))],
+        out_specs=(by_row((rows // n, width)), by_row((rows // n, width)), by_row((q, 128)), by_col((128, 3 * q)), by_row((q, 128)), by_col((128, q)),
                    by_row((q, 128)), by_col((128, ff // n)), by_row((ff // n, 128)), by_col((128, q))),
         compiler_params=pltpu.CompilerParams(vmem_limit_bytes=VMEM_LIMIT),
-        name="expand")(vec, *([gall] * 8), gn, x, gm)
+        name="expand")(vec, *([gall] * 8), gn, x, gm, out)
 
 
 def per_device_fast(tokens, grad_out, segments, padding, adapter_ids, norm1_gain, norm1_bias, w_qkv, w_proj, proj_bias,
@@ -1214,7 +1216,7 @@
     vecf, unused, gm, out, gall, gn = run_block(
         segments, adapter_ids, x, vec, qkv_down, proj_down, proj_up, w_qkv, w_proj, w_fc1, w_fc2, qkv_up,
         grad_out[0], fc1_up, fc1_down, fc2_up, fc2_down)
-    gt, gqd, gqu, gpd, gpu, gf1d, gf1u, gf2d, gf2u = run_expand(vecf, gall, gn, x, gm)
+    out, gt, gqd, gqu, gpd, gpu, gf1d, gf1u, gf2d, gf2u = run_expand(vecf, gall, gn, x, gm, out)
     return out[None], gt[None], gqd, gqu, gpd, gpu, gf1d, gf1u, gf2d, gf2u
 
 

time: 207 us -> 198 us (0.957)
  Pallas kernels: 200 us -> 192 us
  local copies, waits for them, and re-layouts: 3.18 us -> 0.91 us
    pallas_call x1, Pallas kernels: 191 us -> 184 us  [run_block(): pl.pallas_call(block_kernel, out_shape=out_shape, in_specs=[vmem_spec()]...]
    unnamed x1 -> x0, local copies, waits for them, and re-layouts: 2.26 us -> none
where the time goes in v3:
time: 198 us; the launch traced here: 196 us
  Pallas kernels  192 us (97%)
    pallas_call x1, Pallas kernels, run_block(): pl.pallas_call(block_kernel, out_shape=out_shape, in_specs=[vmem_spec()]...  184 us
    pallas_call x1, Pallas kernels, run_expand(): pl.pallas_call(expand_kernel, grid=(n,), out_shape=(sds((rows, width), BF...  7.72 us

profile of v3, /device:TPU:11, one launch (start us, length us, event | category | flops | bytes accessed | tf_op | source)
XLA Modules:
  0.0 195.7 jit_solution(15472041770456316185)
XLA Ops:
  1.3 0.1 pad.3.clone
  1.4 0.1 pad.4.clone
  1.5 0.7 bitcast_convert_fusion
  2.1 0.8 stack.27
  2.9 0.7 maximum_maximum_fusion.vec_ref
  3.6 184.3 %block.1 = (f32[256,128]{1,0:T(8,128)}, bf16[8,640,640]{2,1,0:T(8,128)(2,1)}, f32[512,1024]{1,0:T(8,128)}, bf16[512,1024]{1,0:T(8,128)(2,1)}, bf16[128,16384]{1,0:T(8,128)(2,1)}, /*index=5*/f32[512,1024]{1,0:T(8,128)}) custom-call(s32[1,1024]{1,0:T(1,128)} %seg_ref.1, s32[1,1]{1,0:T(1,128)S(6)} %copy.33.id_ref, bf16[512,1024]{1,0:T(8,128)(2,1)} %bitcast.16, ...), custom_call_target="tpu_custom_call" | custom-call | tf_op jit(solution)/shard_map/block/pallas_call | solution.py:1159
  187.8 7.7 %expand.1 = (bf16[512,1024]{1,0:T(8,128)(2,1)}, f32[512,1024]{1,0:T(8,128)}, f32[1024,128]{1,0:T(8,128)}, f32[128,3072]{1,0:T(8,128)}, f32[1024,128]{1,0:T(8,128...) custom-call(f32[256,128]{1,0:T(8,128)} %get-tuple-element.25.vec_ref, ...), custom_call_target="tpu_custom_call" | custom-call | tf_op jit(solution)/shard_map/expand/pallas_call | solution.py:1193
  (2 shorter events, 0.0 us)

commit v4 on v3

--- a/solution.py
+++ b/solution.py
@@ -856,27 +856,27 @@
             gacc[at, :] += mm_nt(grad_hidden, w1[:, col])
             e3[at, :] += mm_nt(grad_hidden, u1[:, col])
 
-        @pl.when(j + 4 < N_FC1)
-        def _():
-            gather.from_z(fc1_it(j + 4))
-
-        @pl.when(j == 0)
-        def _():
-            gather.from_x(fc1_it(1))
-
-        @pl.when(j + 2 < N_FC1)
-        def _():
-            gather.from_x(fc1_it(j + 2))
-
-        @pl.when(j + 1 < N_FC1)
-        def _():
-            gather.from_seq(fc1_it(j + 1))
-
         gr[:, col] = compact_rows(mm(c3t[...], gh_s[...]))
         gr[:, pl.ds(pl.multiple_of(ff + j * FFB, FFB), FFB)] = compact_rows(mm(e4t[...], act_s[...]))
         for first in (0, ff):
             cols = pl.ds(pl.multiple_of(first + j * FFB, FFB), FFB)
             to_partner(gr.at[:, cols], gr_in.at[:, cols], fs_sem.at[0], fr_sem.at[0]).start()
+
+        @pl.when(j + 4 < N_FC1)
+        def _():
+            gather.from_z(fc1_it(j + 4))
+
+        @pl.when(j == 0)
+        def _():
+            gather.from_x(fc1_it(1))
+
+        @pl.when(j + 2 < N_FC1)
+        def _():
+            gather.from_x(fc1_it(j + 2))
+
+        @pl.when(j + 1 < N_FC1)
+        def _():
+            gather.from_seq(fc1_it(j + 1))
 
     bias2 = full_vector(vecf, 5)
     for n in range(FIRST + N_FC2):
@@ -1004,13 +1004,6 @@
             turn_total(0, parts0).wait_recv()
             dense0[...] = mm(pick, parts0[...]).astype(BF16)
             move("S0", "S1")
-
-        @pl.when(pair == 3)
-        def _():
-            rest_copy.wait_recv()
-            gr_sum[:, cols0:cols0 + cols1] = (gr[:, cols0:cols0 + cols1].astype(F32)
-                                              + gr_in[:, cols0:cols0 + cols1].astype(F32)).astype(BF16)
-            turn_start(1, gr_sum, cols0, parts1, own1)
 
         def cols(part):
             return pl.ds(pl.multiple_of(part * half + pair * 128, 128), 128)
@@ -1045,6 +1038,10 @@
         gq[0:WINDOW, cols(1)] = gk.astype(BF16)
         gq[0:WINDOW, cols(2)] = gv.astype(BF16)
 
+    rest_copy.wait_recv()
+    gr_sum[:, cols0:cols0 + cols1] = (gr[:, cols0:cols0 + cols1].astype(F32)
+                                      + gr_in[:, cols0:cols0 + cols1].astype(F32)).astype(BF16)
+    turn_start(1, gr_sum, cols0, parts1, own1)
     three = slice(0, 3 * half)
     c1[0:WINDOW, :] = (mm_nt(gq[0:WINDOW, three], qu[...]) * image.select_window(0, WINDOW)).astype(BF16)
     up = compact_rows(mm_tn(c1w[...], gq[0:WINDOW, three]))
@@ -1080,13 +1077,18 @@
     move("B0", "S2", "B1")
     turn_total(2, parts2).wait_recv()
     dense2[...] = mm(pick, parts2[...]).astype(BF16)
-    move("S3", "C0", "A2", "C1", "A3", "B2", "C2", "B3")
     gn = oacc
-    for i in range(2):
+
+    def grad_in(i):
         p_copy(i).wait_recv()
         at = slice(i * chunk, (i + 1) * chunk)
         gn[at, :] = prcv[i].astype(F32) + rows_of(s, i).astype(F32)
         put(gn.at[at, :], gn_out.at[at, :])
+
+    move("S3", "C0", "A2", "C1", "A3", "B2")
+    grad_in(0)
+    move("C2", "B3")
+    grad_in(1)
     move("C3")
     for copy in outs:
         copy.wait()

time: 198 us -> 195 us (0.985); the launches traced: 196 us -> 195 us
  no operation moved by 1% of the time
where the time goes in v4:
time: 195 us
  Pallas kernels  191 us (98%)
    pallas_call x1, Pallas kernels, run_block(): pl.pallas_call(block_kernel, out_shape=out_shape, in_specs=[vmem_spec()]...  184 us
    pallas_call x1, Pallas kernels, run_expand(): pl.pallas_call(expand_kernel, grid=(n,), out_shape=(sds((rows, width), BF...  7.72 us

profile of v4, /device:TPU:11, one launch (start us, length us, event | category | flops | bytes accessed | tf_op | source)
XLA Modules:
  0.0 195.2 jit_solution(16158263721421493824)
XLA Ops:
  1.3 0.1 pad.3.clone
  1.4 0.1 pad.4.clone
  1.5 0.7 bitcast_convert_fusion
  2.1 0.8 stack.27
  2.9 0.7 maximum_maximum_fusion.vec_ref
  3.6 183.8 %block.1 = (f32[256,128]{1,0:T(8,128)}, bf16[8,640,640]{2,1,0:T(8,128)(2,1)}, f32[512,1024]{1,0:T(8,128)}, bf16[512,1024]{1,0:T(8,128)(2,1)}, bf16[128,16384]{1,0:T(8,128)(2,1)}, /*index=5*/f32[512,1024]{1,0:T(8,128)}) custom-call(s32[1,1024]{1,0:T(1,128)} %seg_ref.1, s32[1,1]{1,0:T(1,128)S(6)} %copy.33.id_ref, bf16[512,1024]{1,0:T(8,128)(2,1)} %bitcast.16, ...), custom_call_target="tpu_custom_call" | custom-call | tf_op jit(solution)/shard_map/block/pallas_call | solution.py:1161
  187.3 7.7 %expand.1 = (bf16[512,1024]{1,0:T(8,128)(2,1)}, f32[512,1024]{1,0:T(8,128)}, f32[1024,128]{1,0:T(8,128)}, f32[128,3072]{1,0:T(8,128)}, f32[1024,128]{1,0:T(8,128...) custom-call(f32[256,128]{1,0:T(8,128)} %get-tuple-element.25.vec_ref, ...), custom_call_target="tpu_custom_call" | custom-call | tf_op jit(solution)/shard_map/expand/pallas_call | solution.py:1195
  (2 shorter events, 0.0 us)

commit v5 on v4

--- a/solution.py
+++ b/solution.py
@@ -592,10 +592,10 @@
 N_ITEMS = FIRST + N_FC2 + N_FC1
 
 
-def block_kernel(seg_ref, id_ref, x_ref, vec_ref, qd_ref, pd_ref, pu_ref, wq_hbm, wp_hbm, w1_hbm, w2_hbm,
+def block_kernel(seg_ref, id_ref, vec_ref, x_hbm, qd_hbm, pd_hbm, pu_hbm, wq_hbm, wp_hbm, w1_hbm, w2_hbm,
                  qu_hbm, g_hbm, u1_hbm, d1_hbm, u2_hbm, d2_hbm,
                  vecf_out, prob_out, gm_out, out_out, gall, gn_out,
-                 wq_own, wq, wp, w1, w2, xp, vecf, qu, g, u1, d1, u2, d2, qkv, n1, c1, qkvw, n1w, c1w, prob, opad, sendb,
+                 x_ref, qd_ref, pd_ref, pu_ref, wq_own, wq, wp, w1, w2, xp, vecf, qu, g, u1, d1, u2, d2, qkv, n1, c1, qkvw, n1w, c1w, prob, opad, sendb,
                  oh, att, c2, mid, n2, oacc, gacc, u4, e3, c3, e4, c3t, e4t, act_s, gh_s, gr,
                  do_s, gr_in, gr_sum, last_own, last_in, last_sum, parts0, parts1, parts2, dense0, dense1, dense2, prcv,
                  xs_sem, xr_sem, as_sem, ar_sem, loc_sem, out_sem, prob_sem, g_sem, g_own,
@@ -618,7 +618,8 @@
     for part in range(3):
         cols = pl.ds(pl.multiple_of(part * width + s * half, 128), half)
         late.append(pltpu.make_async_copy(qu_hbm.at[:, cols], qu.at[:, pl.ds(part * half, half)], loc_sem.at[3 + part]))
-    for n, (src, dst) in enumerate(((g_hbm, g), (u1_hbm, u1), (d1_hbm, d1), (u2_hbm, u2), (d2_hbm, d2))):
+    for n, (src, dst) in enumerate(((x_hbm, x_ref), (qd_hbm, qd_ref), (g_hbm, g), (u1_hbm, u1), (d1_hbm, d1),
+                                  (u2_hbm, u2), (d2_hbm, d2), (pd_hbm, pd_ref), (pu_hbm, pu_ref))):
         late.append(pltpu.make_async_copy(src, dst, loc_sem.at[6 + n]))
     for copy in pre + late:
         copy.start()
@@ -627,7 +628,7 @@
     def x_copy(i):
         part = pl.ds(i * chunk, chunk)
         return pltpu.make_async_remote_copy(
-            src_ref=x_ref.at[part, :], dst_ref=xp.at[part, :], send_sem=xs_sem.at[i], recv_sem=xr_sem.at[i],
+            src_ref=x_hbm.at[part, :], dst_ref=xp.at[part, :], send_sem=xs_sem.at[i], recv_sem=xr_sem.at[i],
             device_id=net.partner, device_id_type=MESH)
 
     for i in range(2):
@@ -1145,7 +1146,7 @@
         return pltpu.VMEM(shape, F32)
 
     scratch = [
-        low(wq.shape[0], 3 * half), low(width, 3 * half), low(width, width), low(width, ff), low(ff, width),
+        low(rows, width), low(width, 128), low(width, 128), low(128, width), low(wq.shape[0], 3 * half), low(width, 3 * half), low(width, width), low(width, ff), low(ff, width),
         low(rows, width), full(256, 128), low(128, 3 * half), low(rows, width), low(128, ff), low(width, 128),
         low(128, width), low(ff, 128), low(toks, 3 * half), low(toks, width), low(toks, 128),
         low(WINDOW, 3 * half), low(WINDOW, width), low(WINDOW, 128), low(2, 2, WINDOW, WINDOW), low(2 * PAD + WINDOW, 128),
@@ -1155,14 +1156,14 @@
         low(toks, half), low(16, gcols), low(16, gcols), low(16, last), low(16, last), low(16, last),
         low(256, 2 * ff // 16), low(256, last // 16), low(256, last // 16), low(128, 2 * ff // 16), low(128, last // 16),
         low(128, last // 16), low(2, chunk, width),
-        dma((2,)), dma((2,)), dma((4,)), dma((4,)), dma((11,)), dma((12,)), dma((2,)),
+        dma((2,)), dma((2,)), dma((4,)), dma((4,)), dma((15,)), dma((12,)), dma((2,)),
         dma((N_SEMS, N_ITEMS + 4)), dma((N_ITEMS + 4,)),
         dma((4,)), dma((4,)), dma((3,)), dma((3,)), dma((2,)), dma((2,)), dma((3,)), dma((3,))]
     return pl.pallas_call(
-        block_kernel, out_shape=out_shape, in_specs=[vmem_spec()] * 7 + [any_spec()] * 10,
+        block_kernel, out_shape=out_shape, in_specs=[vmem_spec()] * 3 + [any_spec()] * 14,
         out_specs=tuple(any_spec() for unused in out_shape), scratch_shapes=scratch,
         compiler_params=pltpu.CompilerParams(collective_id=1, has_side_effects=True, vmem_limit_bytes=VMEM_LIMIT),
-        name="block")(seg, ident, x, vec, qd, pd, pu, wq, wp, w1, w2, qu, g, u1, d1, u2, d2)
+        name="block")(seg, ident, vec, x, qd, pd, pu, wq, wp, w1, w2, qu, g, u1, d1, u2, d2)
 
 
 def expand_kernel(vec_ref, f1u, f2d, f1d, f2u, pu, pdn, qu, qd, gn, x, gm, out,

time: 195 us -> 195 us (level)
  no operation moved by 1% of the time
where the time goes in v5:
time: 195 us
  Pallas kernels  191 us (98%)
    pallas_call x1, Pallas kernels, run_block(): pl.pallas_call(block_kernel, out_shape=out_shape, in_specs=[vmem_spec()]...  183 us
    pallas_call x1, Pallas kernels, run_expand(): pl.pallas_call(expand_kernel, grid=(n,), out_shape=(sds((rows, width), BF...  7.72 us

profile of v5, /device:TPU:11, one launch (start us, length us, event | category | flops | bytes accessed | tf_op | source)
XLA Modules:
  0.0 194.6 jit_solution(11472194121484358957)
XLA Ops:
  1.3 0.1 pad.3.clone
  1.4 0.1 pad.4.clone
  1.5 0.7 bitcast_convert_fusion
  2.1 0.8 stack.27
  2.9 0.7 maximum_maximum_fusion.vec_ref
  3.6 183.2 %block.1 = (f32[256,128]{1,0:T(8,128)}, bf16[8,640,640]{2,1,0:T(8,128)(2,1)}, f32[512,1024]{1,0:T(8,128)}, bf16[512,1024]{1,0:T(8,128)(2,1)}, bf16[128,16384]{1,0:T(8,128)(2,1)}, /*index=5*/f32[512,1024]{1,0:T(8,128)}) custom-call(s32[1,1024]{1,0:T(1,128)} %seg_ref.1, s32[1,1]{1,0:T(1,128)S(6)} %copy.33.id_ref, f32[16,128]{1,0:T(8,128)} %maximum_maximum_fusion.vec_ref, ...), custom_call_target="tpu_custom_call" | custom-call | tf_op jit(solution)/shard_map/block/pallas_call | solution.py:1162
  186.7 7.7 %expand.1 = (bf16[512,1024]{1,0:T(8,128)(2,1)}, f32[512,1024]{1,0:T(8,128)}, f32[1024,128]{1,0:T(8,128)}, f32[128,3072]{1,0:T(8,128)}, f32[1024,128]{1,0:T(8,128...) custom-call(f32[256,128]{1,0:T(8,128)} %get-tuple-element.25.vec_ref, ...), custom_call_target="tpu_custom_call" | custom-call | tf_op jit(solution)/shard_map/expand/pallas_call | solution.py:1196
  (2 shorter events, 0.0 us)
